TPU v7x, 512 devices: a whole 4x8x8 slice. The times are simulated.
512 devices in a mesh: dp: 64 (over y, x, z_lo), feat: 8 (over z_hi, core).
Axes of the slice: x: 4, y: 8, z: 8 (z_hi: 4, z_lo: 2; z = z_hi * 2 + z_lo), core: 2. Of those that a mesh axis runs over, the one named last changes fastest.
Arguments:
- embeddings: bfloat16 [327680, 2048], P('dp', 'feat'), may hold values from -80 to 80
- slot_image: int32 [327680], P('dp'), may hold values from 0 to 32767, as said below
- slot_view: int32 [327680], P('dp'), may hold values from 0 to 10, as said below
- pair_table: int32 [2, 2], replicated, may hold values from 0 to 9, as said below
Outputs:
- correlation: float32 [2, 2048, 2048], P(None, 'feat', 'dp')
Inputs may be any that keep to these rules, and one draw needn't show every extreme that they name: `slot_image`: image ids of dp index d run from d * 512 to (d + 1) * 512 - 1. Each image has views 0 and 1 and local views 2 to 1 + k with k from 1 to 8; the first image of every dp index has all 10 views; every (image, view) stands in one slot at most; empty slots name an image of their own dp index. `slot_view`: empty slots carry view 10 and come after the used slots of their dp index; the last dp index fills all its slots. `pair_table`: each pair's first view is global (0 or 1) and its second view differs from it.
All inputs are finite; a program needn't handle non-finite values.
Results may differ from a plain program's by a relative error of at most 0.00035.
Values may be sent and summed in bfloat16 or wider, within the bound.
A program may use at most 64 MiB of HBM per device.

v0:
```python
import jax
import jax.numpy as jnp
from jax import lax
from jax.sharding import Mesh
from jax.sharding import PartitionSpec as P

WIN = 2048
IMG_DEV = 512
PAIRS = 2
FEAT = ("feat_0", "feat_1")
DP = ("dp_0", "dp_1", "dp_2")
DP_FEAT = ("dp_0", "dp_1", "dp_2", "feat_0", "feat_1")


EPS = 1e-05


def one_axis_at_a_time(array, axes):
    for axis in axes:
        array = lax.psum(array, axis)
    return array


def split_up(array, dim, peers):
    before, after = (array.shape[:dim], array.shape[dim + 1 :])
    return jnp.moveaxis(array.reshape(*before, peers, -1, *after), dim, 0)


def summed_on_arrival(array, axis, dim):
    parts = split_up(array, dim, lax.axis_size(axis))
    arrived = lax.all_to_all(parts, axis, split_axis=0, concat_axis=0, tiled=True)
    return arrived.sum(axis=0)


def select_rows(embeddings, local_image, slot_view, view_id):
    image_grid = jnp.arange(IMG_DEV, dtype=jnp.int32)[:, None]
    selection = ((local_image[None, :] == image_grid) & (slot_view[None, :] == view_id)).astype(
        jnp.bfloat16
    )
    found = jnp.sum(selection.astype(jnp.float32), axis=1) > 0.5
    rows = jnp.dot(selection, embeddings, preferred_element_type=jnp.float32).astype(jnp.bfloat16)
    return (rows, found)


def image_product(columns, first_rows):
    return lax.dot_general(
        columns, first_rows, (((0,), (0,)), ((), ())), preferred_element_type=jnp.float32
    )


def local(embeddings, slot_image, slot_view, pair_table):
    width_local = embeddings.shape[1]
    feat_offset = lax.axis_index(FEAT) * width_local
    out_rows = WIN // lax.axis_size(DP)
    dp_offset = lax.axis_index(DP) * out_rows
    local_image = slot_image - lax.axis_index(DP) * IMG_DEV
    zeros_wide = jnp.zeros((WIN,), jnp.float32)
    outputs = []
    for pair_index in range(PAIRS):
        first_taken, first_found = select_rows(
            embeddings, local_image, slot_view, pair_table[pair_index, 0]
        )
        second_taken, second_found = select_rows(
            embeddings, local_image, slot_view, pair_table[pair_index, 1]
        )
        present = first_found & second_found
        first_rows = jnp.where(present[:, None], first_taken, jnp.zeros((), jnp.bfloat16))
        second_rows = jnp.where(present[:, None], second_taken, jnp.zeros((), jnp.bfloat16))
        first_wide = first_rows.astype(jnp.float32)
        second_wide = second_rows.astype(jnp.float32)
        images_here = jnp.sum(present.astype(jnp.float32))
        images_term = jnp.where(lax.axis_index(FEAT) == 0, images_here, jnp.zeros((), jnp.float32))

        def widen(vector):
            return lax.dynamic_update_slice_in_dim(zeros_wide, vector, feat_offset, 0)

        sum_first, sumsq_first, sum_second, sumsq_second, total = (
            one_axis_at_a_time(widen(jnp.sum(first_wide, axis=0)), DP_FEAT),
            one_axis_at_a_time(widen(jnp.sum(first_wide * first_wide, axis=0)), DP_FEAT),
            one_axis_at_a_time(widen(jnp.sum(second_wide, axis=0)), DP_FEAT),
            one_axis_at_a_time(widen(jnp.sum(second_wide * second_wide, axis=0)), DP_FEAT),
            one_axis_at_a_time(images_term, DP_FEAT),
        )
        partial_value = image_product(
            lax.all_gather(second_rows, FEAT, axis=1, tiled=True), first_rows
        )
        reduced = summed_on_arrival(partial_value, DP, 0)
        mean_first = lax.dynamic_slice_in_dim(sum_first, feat_offset, width_local, 0) / total
        square_first = lax.dynamic_slice_in_dim(sumsq_first, feat_offset, width_local, 0) / total
        mean_second = lax.dynamic_slice_in_dim(sum_second, dp_offset, out_rows, 0) / total
        square_second = lax.dynamic_slice_in_dim(sumsq_second, dp_offset, out_rows, 0) / total
        spread_first = jnp.sqrt(square_first - mean_first * mean_first + EPS)
        spread_second = jnp.sqrt(square_second - mean_second * mean_second + EPS)
        cross = reduced.T
        block = (cross / total - mean_first[:, None] * mean_second[None, :]) / (
            spread_first[:, None] * spread_second[None, :]
        )
        outputs.append(block)
    return jnp.stack(outputs, axis=0)


def solution(mesh):
    split = Mesh(mesh.devices.reshape(8, 4, 2, 4, 2), ("dp_0", "dp_1", "dp_2", "feat_0", "feat_1"))
    placed = (P(DP, FEAT), P(DP), P(DP), P())
    return jax.shard_map(
        local, mesh=split, in_specs=placed, out_specs=P(None, FEAT, DP), check_vma=False
    )
```

profile of v0, /device:TPU:6, one launch (start us, length us, event | category | flops | bytes accessed | tf_op | source)
XLA Modules:
  0.0 291.9 jit_solution(17913414915544847246)
XLA Ops:
  6.5 1.5 fusion.56
  8.0 0.7 broadcast_subtract_fusion
  8.7 3.3 %broadcast_compare_fusion.2 = (pred[5120]{0:T(1024)(128)(4,1)S(1)}, pred[5120]{0:T(1024)(128)(4,1)S(1)}, pred[5120]{0:T(1024)(128)(4,1)S(1)}, pred[5120]{0:T(1024)(128)(4,1)S(1)}) fusion(s32[5120]{0:T(1024)} %param.6, s32[]{:T(128)} %bitcast.1, s32[]{:T(128)} %bitcast, s32[]{:T(128)} %bitcast.6, s32[]{:T(128)} %bitcast.5), kind=kLoop, calls=%fused_computation.54 | loop fusion | flops 20480 | bytes 40976 | tf_op jit(solution)/shard_map/eq | solution.py:37
  12.0 5.7 %convert_reduce_fusion.3 = (f32[512]{0:T(512)S(1)}, f32[512]{0:T(512)S(1)}, f32[512]{0:T(512)S(1)}, f32[512]{0:T(512)S(1)}) fusion(s32[5120]{0:T(1024)S(1)} %broadcast_subtract_fusion, pred[5120]{0:T(1024)(128)(4,1)S(1)} %get-tuple-element.80, pred[5120]{0:T(1024)(128)(4,1)S(1)} %get-tuple-element.81, pred[5120]{0:T(1024)(128)(4,1)S(1)} %get-tuple-element.82, ...), kind=kLoop, calls=%fused_computation.3 | loop fusion | flops 44562432 | bytes 49152 | tf_op jit(solution)/shard_map/reduce_sum | solution.py:40
  17.7 0.6 convert_reduce_fusion.8
  18.3 2.8 fusion.51
  21.1 2.0 fusion.50
  23.1 46.8 %all-gather.5.cloned.1.call-done = bf16[512,2048]{1,0:T(8,128)(2,1)} async-done(((bf16[512,256]{1,0:T(8,128)(2,1)}), bf16[512,2048]{1,0:T(8,128)(2,1)}) %all-gather.5.cloned.1.call-update) | async-done | bytes 2097168 | tf_op jit(solution)/shard_map/all_gather | solution.py:85
  69.9 3.7 %fusion.58 = f32[2048,256]{1,0:T(8,128)} fusion(bf16[512,2048]{1,0:T(8,128)(2,1)} %all-gather.5.cloned.1.call-done, bf16[512,256]{1,0:T(8,128)(2,1)S(1)} %get-tuple-element.88), kind=kOutput, calls=%fused_computation.75 | convolution fusion | flops 536870912 | bytes 4456448 | tf_op jit(solution)/shard_map/dot_general | solution.py:46
  73.6 10.4 %all-to-all-start.1 = ((f32[64,32,256]{2,1,0:T(8,128)}), f32[64,32,256]{2,1,0:T(8,128)}, u32[]{:S(2)}, u32[]{:S(2)}) async-start(f32[64,32,256]{2,1,0:T(8,128)} %bitcast.31), calls=%async_computation.1 | async-start | bytes 4194304 | tf_op jit(solution)/shard_map/all_to_all | solution.py:31
  84.3 2.8 fusion.49
  87.1 2.0 fusion.48
  89.1 50.2 %all-gather.3.cloned.1.call-done = bf16[512,2048]{1,0:T(8,128)(2,1)} async-done(((bf16[512,256]{1,0:T(8,128)(2,1)}), bf16[512,2048]{1,0:T(8,128)(2,1)}) %all-gather.3.cloned.1.call-update) | async-done | bytes 2097168 | tf_op jit(solution)/shard_map/all_gather | solution.py:85
  139.3 3.6 %fusion.57 = f32[2048,256]{1,0:T(8,128)} fusion(bf16[512,2048]{1,0:T(8,128)(2,1)} %all-gather.3.cloned.1.call-done, bf16[512,256]{1,0:T(8,128)(2,1)S(1)} %get-tuple-element.90), kind=kOutput, calls=%fused_computation.74 | convolution fusion | flops 536870912 | bytes 4456448 | tf_op jit(solution)/shard_map/dot_general | solution.py:46
  142.9 10.0 %all-to-all-start = ((f32[64,32,256]{2,1,0:T(8,128)}), f32[64,32,256]{2,1,0:T(8,128)}, u32[]{:S(2)}, u32[]{:S(2)}) async-start(f32[64,32,256]{2,1,0:T(8,128)} %bitcast.30), calls=%async_computation | async-start | bytes 4194304 | tf_op jit(solution)/shard_map/all_to_all | solution.py:31
  152.9 0.3 dynamic_update_slice.29
  153.2 0.3 dynamic_update_slice.31
  155.5 0.3 dynamic_update_slice.27
  156.3 68.0 %all-reduce.10 = (f32[2048]{0:T(1024)S(1)}, f32[]{:T(128)}, f32[2048]{0:T(1024)S(1)}, f32[2048]{0:T(1024)S(1)}, f32[2048]{0:T(1024)S(1)}, /*index=5*/f32[2048]{0...) all-reduce(f32[2048]{0:T(1024)S(1)} %dynamic_update_slice.29, ...), channel_id=1, replica_groups=mesh['dp_0'=8,'dp_1'=4,'dp_2'=2,'feat_0'=4,'feat_1'=2] {'dp_0'}, use_global_device_ids=true, to_apply=%region_49.50 | all-reduce | flops 16386 | bytes 131088 | tf_op jit(solution)/shard_map/psum | solution.py:20
  224.3 15.3 %all-reduce.11 = (f32[2048]{0:T(1024)S(1)}, f32[]{:T(128)}, f32[2048]{0:T(1024)S(1)}, f32[2048]{0:T(1024)S(1)}, f32[2048]{0:T(1024)S(1)}, /*index=5*/f32[2048]{0...) all-reduce(f32[2048]{0:T(1024)S(1)} %get-tuple-element.17, ...), channel_id=1, replica_groups=mesh['dp_0'=8,'dp_1'=4,'dp_2'=2,'feat_0'=4,'feat_1'=2] {'dp_1'}, use_global_device_ids=true, to_apply=%region_50.51 | all-reduce | flops 16386 | bytes 131088 | tf_op jit(solution)/shard_map/psum | solution.py:20
  239.6 10.2 %all-reduce.12 = (f32[2048]{0:T(1024)S(1)}, f32[]{:T(128)}, f32[2048]{0:T(1024)S(1)}, f32[2048]{0:T(1024)S(1)}, f32[2048]{0:T(1024)S(1)}, /*index=5*/f32[2048]{0...) all-reduce(f32[2048]{0:T(1024)S(1)} %get-tuple-element.37, ...), channel_id=1, replica_groups=mesh['dp_0'=8,'dp_1'=4,'dp_2'=2,'feat_0'=4,'feat_1'=2] {'dp_2'}, use_global_device_ids=true, to_apply=%region_51.52 | all-reduce | flops 16386 | bytes 131088 | tf_op jit(solution)/shard_map/psum | solution.py:20
  249.8 22.2 %all-reduce.13 = (f32[2048]{0:T(1024)S(1)}, f32[]{:T(128)}, f32[2048]{0:T(1024)S(1)}, f32[2048]{0:T(1024)S(1)}, f32[2048]{0:T(1024)S(1)}, /*index=5*/f32[2048]{0...) all-reduce(f32[2048]{0:T(1024)S(1)} %get-tuple-element.57, ...), channel_id=1, replica_groups=mesh['dp_0'=8,'dp_1'=4,'dp_2'=2,'feat_0'=4,'feat_1'=2] {'feat_0'}, use_global_device_ids=true, to_apply=%region_52.53 | all-reduce | flops 16386 | bytes 131088 | tf_op jit(solution)/shard_map/psum | solution.py:20
  272.0 4.8 %all-reduce.14 = (f32[2048]{0:T(1024)S(1)}, f32[]{:T(128)}, f32[2048]{0:T(1024)S(1)}, f32[2048]{0:T(1024)S(1)}, f32[2048]{0:T(1024)S(1)}, /*index=5*/f32[2048]{0...) all-reduce(f32[2048]{0:T(1024)S(1)} %get-tuple-element.27, ...), channel_id=1, replica_groups=mesh['dp_0'=8,'dp_1'=4,'dp_2'=2,'feat_0'=4,'feat_1'=2] {'feat_1'}, use_global_device_ids=true, to_apply=%region_53.54 | all-reduce | flops 16386 | bytes 131088 | tf_op jit(solution)/shard_map/psum | solution.py:20
  276.8 0.7 add_sqrt_fusion.2
  277.5 0.7 add_sqrt_fusion.3
  278.2 0.7 add_sqrt_fusion
  278.9 0.7 add_sqrt_fusion.1
  279.6 1.7 reduce_sum.154
  281.3 0.7 fusion.53
  282.1 1.7 reduce_sum.146
  283.8 0.7 fusion.55
  284.5 0.6 pad_maximum_fusion
  (21 shorter events, 1.6 us)
Async XLA Ops:
  6.5 11.7 %copy-start = (bf16[5120,256]{1,0:T(8,128)(2,1)S(1)}, bf16[5120,256]{1,0:T(8,128)(2,1)}, u32[]{:S(2)}) copy-start(bf16[5120,256]{1,0:T(8,128)(2,1)} %param.4) | copy-start | bytes 7864324
  6.5 63.4 %all-gather.5.cloned.1.call-start = ((), (), s32[]{:S(2)}) async-start(), calls=%async_computation.3 | async-start | bytes 2359296 | tf_op jit(solution)/shard_map/all_gather | solution.py:85
  73.6 69.3 %all-to-all-start.1 = ((f32[64,32,256]{2,1,0:T(8,128)}), f32[64,32,256]{2,1,0:T(8,128)}, u32[]{:S(2)}, u32[]{:S(2)}) async-start(f32[64,32,256]{2,1,0:T(8,128)} %bitcast.31), calls=%async_computation.1 | async-start | bytes 4194304 | tf_op jit(solution)/shard_map/all_to_all | solution.py:31
  84.1 55.3 %all-gather.3.cloned.1.call-start = ((), (), s32[]{:S(2)}) async-start(), calls=%async_computation.2 | async-start | bytes 2359296 | tf_op jit(solution)/shard_map/all_gather | solution.py:85
  142.9 139.1 %all-to-all-start = ((f32[64,32,256]{2,1,0:T(8,128)}), f32[64,32,256]{2,1,0:T(8,128)}, u32[]{:S(2)}, u32[]{:S(2)}) async-start(f32[64,32,256]{2,1,0:T(8,128)} %bitcast.30), calls=%async_computation | async-start | bytes 4194304 | tf_op jit(solution)/shard_map/all_to_all | solution.py:31
Sparse Core Ops, SparseCore 0:
  21.2 48.7 all-gather.4
  87.2 52.0 all-gather.2
where the time goes:
time: 297 us; the launch traced here: 292 us
  blocking collectives  120 us (40%)
  waiting for transfers between devices  97.1 us (33%)
  starting transfers between devices  20.6 us (7%)
  other arithmetic  18.5 us (6%)
  matrix products  16.9 us (6%)
  between operations  14.7 us (5%)
  local copies, waits for them, and re-layouts  3.62 us (1%)
    psum x5, blocking collectives, one_axis_at_a_time(): array = lax.psum(array, axis)  120 us
    all_gather x2, waiting for transfers between devices, local(): lax.all_gather(second_rows, FEAT, axis=1, tiled=True)  97 us
    all_to_all x2, starting transfers between devices, summed_on_arrival(): lax.all_to_all(parts, axis, split_axis=0, concat_axis=0, tiled=True)  20.4 us
    dot_general x4, matrix products, select_rows(): jnp.dot(selection, embeddings, preferred_element_type=jnp.float32)  9.6 us
    dot_general x2, matrix products, image_product(): lax.dot_general(columns, first_rows, (((0,), (0,)), ((), ())), preferred_...  7.29 us
  transfers between devices with their start and end apart: 4, of which 2 were waited for; matrix products, arithmetic and copies ran while one was open for 6% of the time, Pallas kernels for 0%

commit v1 on v0

v1 whole, which is shorter than its diff:
```python
import jax
import jax.numpy as jnp
from jax import lax
from jax.experimental import pallas as pl
from jax.experimental.pallas import tpu as pltpu
from jax.sharding import Mesh
from jax.sharding import PartitionSpec as P

WIN = 2048
IMG_DEV = 512
PAIRS = 2
WIDTH = 256
OWN = 32
NX, NY = 4, 8
BLOCK = 64
STAT = 8
ROWS = BLOCK + STAT
PART = OWN + STAT
CUT = 40
SLOTS = 1024
VIEW_STRIDE = 16
AXES = ("y", "x", "zl", "zh", "core")
FEAT = ("zh", "core")
DP = ("y", "x", "zl")
EPS = 1e-05
F32 = jnp.float32
BF16 = jnp.bfloat16
MESH = pl.DeviceIdType.MESH


def select_kernel(pair_ref, image_ref, view_ref, emb_ref, x1_ref, x2_ref, stat_ref, acc, found):
    step = pl.program_id(0)

    @pl.when(step == 0)
    def _():
        acc[...] = jnp.zeros_like(acc)
        found[...] = jnp.zeros_like(found)

    base = lax.axis_index(DP) * IMG_DEV
    key = image_ref[...] * VIEW_STRIDE + view_ref[...]
    wanted = (lax.broadcasted_iota(jnp.int32, (IMG_DEV, 128), 0) + base) * VIEW_STRIDE
    for pair in range(PAIRS):
        for side in range(2):
            target = wanted + pair_ref[pair, side]
            hits = [
                jnp.where(key[row : row + 1, :] == target, 1.0, 0.0) for row in range(SLOTS // 128)
            ]
            chosen = jnp.concatenate([hit.astype(BF16) for hit in hits], axis=1)
            acc[2 * pair + side] += jnp.dot(chosen, emb_ref[...], preferred_element_type=F32)
            if side == 1:
                found[pair] += sum(hits[1:], hits[0])

    @pl.when(step == pl.num_programs(0) - 1)
    def _():
        row = lax.broadcasted_iota(jnp.int32, (STAT, WIDTH), 0)
        for pair in range(PAIRS):
            present = jnp.sum(found[pair], axis=1, keepdims=True)
            x1_ref[pair] = jnp.where(present > 0.5, acc[2 * pair], 0.0).astype(BF16)
            second = acc[2 * pair + 1]
            x2_ref[pair] = second.T.astype(BF16)
            total = jnp.sum(second, axis=0, keepdims=True)
            square = jnp.sum(second * second, axis=0, keepdims=True)
            count = jnp.sum(present)
            stat_ref[pair] = jnp.where(
                row == 2, total, jnp.where(row == 3, square, jnp.where(row == 4, count, 0.0))
            )


def select(pair_table, slot_image, slot_view, embeddings):
    slots = embeddings.shape[0]
    steps = slots // SLOTS
    ids = pl.BlockSpec((SLOTS // 128, 128), lambda k: (k, 0))
    whole = lambda *shape: pl.BlockSpec(shape, lambda k: (0,) * len(shape))
    return pl.pallas_call(
        select_kernel,
        grid=(steps,),
        out_shape=(
            jax.ShapeDtypeStruct((PAIRS, IMG_DEV, WIDTH), BF16),
            jax.ShapeDtypeStruct((PAIRS, WIDTH, IMG_DEV), BF16),
            jax.ShapeDtypeStruct((PAIRS, STAT, WIDTH), F32),
        ),
        in_specs=[
            pl.BlockSpec(memory_space=pltpu.SMEM),
            ids,
            ids,
            pl.BlockSpec((SLOTS, WIDTH), lambda k: (k, 0)),
        ],
        out_specs=(
            whole(PAIRS, IMG_DEV, WIDTH),
            whole(PAIRS, WIDTH, IMG_DEV),
            whole(PAIRS, STAT, WIDTH),
        ),
        scratch_shapes=[
            pltpu.VMEM((2 * PAIRS, IMG_DEV, WIDTH), F32),
            pltpu.VMEM((PAIRS, IMG_DEV, 128), F32),
        ],
        name="select",
    )(pair_table, slot_image.reshape(slots // 128, 128), slot_view.reshape(slots // 128, 128), embeddings)


def shift_of(plane, core):
    return 7 + core + 4 * (plane // 2)


def cross_kernel(
    x1_ref, x2_ref, stat_ref, out_ref,
    x1p, x1a, x1ap, x2b, statb, x1stat, cb, relay_p, relay_m, from_m, from_p, total, yr, fs, fr,
    z_send, z_recv, x_send, x_recv, y_send, y_recv, f_send, f_recv,
):
    y, x, zl, h, core = [lax.axis_index(axis) for axis in AXES]
    plane_a = h + 1 - 2 * (h % 2)
    plane_b = 3 - h
    other = 1 - core
    xp, xa, xm = (x + 1) % NX, (x + 2) % NX, (x + 3) % NX
    yp, ym = (y + 1) % NY, (y + NY - 1) % NY
    mine = (y + 2 * NY - shift_of(h, core)) % NY

    jb, ih, half = mine // 4, (mine // 2) % 2, mine % 2
    owner_y = 2 * (h + jb * (3 - 2 * h)) + core
    owner_h = h + ih * (1 - 2 * (h % 2))
    at_home = (owner_y == y) & (owner_h == h) & (half == core)
    jh, src_core = y // 2, y % 2
    src_jb = (jh // 2 + h // 2) % 2
    src_h = jh + src_jb * (3 - 2 * jh)
    src_ih = (src_h + h) % 2
    src_y = (4 * src_jb + 2 * src_ih + core + shift_of(src_h, src_core)) % NY

    barrier = pltpu.get_barrier_semaphore()
    for peer in ({"x": xp}, {"x": xm}, {"y": yp}, {"y": ym}, {"zh": plane_a}, {"zh": plane_b}, {"core": other}):
        pl.semaphore_signal(barrier, inc=1, device_id=peer, device_id_type=MESH)
    for part in range(2):

        @pl.when(jnp.logical_not(at_home & (zl == part)))
        def _():
            pl.semaphore_signal(
                barrier,
                inc=1,
                device_id={"y": src_y, "zl": part, "zh": src_h, "core": src_core},
                device_id_type=MESH,
            )

    pl.semaphore_wait(barrier, 9 - at_home.astype(jnp.int32))

    sent = []

    def send(src, dst, send_sem, recv_sem, peer):
        copy = pltpu.make_async_remote_copy(
            src_ref=src, dst_ref=dst, send_sem=send_sem, recv_sem=recv_sem, device_id=peer, device_id_type=MESH
        )
        copy.start()
        sent.append(copy)
        return copy

    z = {}
    for pair in range(PAIRS):
        for slot, (name, src, dst, peer) in enumerate(
            (
                ("p", x1_ref, x1p, {"core": other}),
                ("b", x2_ref, x2b, {"zh": plane_b}),
                ("s", stat_ref, statb, {"zh": plane_b}),
                ("a", x1_ref, x1a, {"zh": plane_a}),
            )
        ):
            z[name, pair] = send(src.at[pair], dst.at[pair], z_send.at[pair, slot], z_recv.at[pair, slot], peer)

    def forward(pair):
        z["a", pair].wait_recv()
        z["ap", pair] = send(
            x1a.at[pair], x1ap.at[pair], z_send.at[pair, 4], z_recv.at[pair, 4], {"core": other}
        )

    stats_done = set()
    xc = {}

    def block_of(pair, jb, ih):
        return 4 * pair + 2 * jb + ih

    def multiply(pair, jb, ih):
        k = block_of(pair, jb, ih)
        second = (x2b if jb else x2_ref)[pair]
        stat = (statb if jb else stat_ref)[pair]
        row = lax.broadcasted_iota(jnp.int32, (STAT, WIDTH), 0)
        for slot, (ref, half) in enumerate((((x1a if ih else x1_ref), core), ((x1ap if ih else x1p), other))):
            first = ref[pair]
            if (pair, ih, slot) not in stats_done:
                stats_done.add((pair, ih, slot))
                wide = first.astype(F32)
                plain = jnp.sum(wide, axis=0, keepdims=True)
                square = jnp.sum(wide * wide, axis=0, keepdims=True)
                x1stat[pair, ih, slot] = jnp.where(row == 0, plain, jnp.where(row == 1, square, 0.0))
            product = jnp.dot(second, first, preferred_element_type=F32)
            sums = x1stat[pair, ih, slot] + stat
            for dest in range(NX):
                cb[k, dest, half, 0:BLOCK] = product[dest * BLOCK : (dest + 1) * BLOCK]
                cb[k, dest, half, BLOCK:ROWS] = sums
        for slot, (src, dst, to) in enumerate(
            (
                (cb.at[k, xa, 0], relay_p.at[k], xp),
                (cb.at[k, xa, 1], relay_m.at[k], xm),
                (cb.at[k, xp, 1], from_m.at[k, 1], xp),
                (cb.at[k, xm, 0], from_p.at[k, 0], xm),
            )
        ):
            xc[k, slot] = send(src, dst, x_send.at[k, slot], x_recv.at[k, slot], {"x": to})

    def pass_on(pair, jb, ih):
        k = block_of(pair, jb, ih)
        xc[k, 0].wait_recv()
        cb[k, xp, 0] += relay_p[k]
        xc[k, 4] = send(cb.at[k, xp, 0], from_m.at[k, 0], x_send.at[k, 4], x_recv.at[k, 4], {"x": xp})
        xc[k, 1].wait_recv()
        cb[k, xm, 1] += relay_m[k]
        xc[k, 5] = send(cb.at[k, xm, 1], from_p.at[k, 1], x_send.at[k, 5], x_recv.at[k, 5], {"x": xm})

    def collect(pair, jb, ih):
        k = block_of(pair, jb, ih)
        for slot in (2, 3, 4, 5):
            xc[k, slot].wait_recv()
        for half in range(2):
            total[pair, 4 * jb + 2 * ih + half] = cb[k, x, half] + from_m[k, half] + from_p[k, half]

    yc = {}

    def y_send_part(pair, way, step, src, dst):
        to = ym if way else yp
        yc[pair, way, step] = send(
            src, dst, y_send.at[pair, way, step], y_recv.at[pair, way, step], {"y": to}
        )

    def y_step(pair, step):
        for way in range(2):
            ahead = (mine + (4 + step if way else 4 - step)) % NY
            rows = slice(CUT, ROWS) if way else slice(0, CUT)
            size = ROWS - CUT if way else CUT
            if step == 0:
                y_send_part(pair, way, 0, total.at[pair, ahead, rows], yr.at[pair, way, 0, 0:size])
                continue
            yc[pair, way, step - 1].wait_recv()
            if step == 1:
                total[pair, ahead, rows] += yr[pair, way, 0, 0:size]
            else:
                total[pair, ahead] += yr[pair, way, step - 1]
            y_send_part(pair, way, step, total.at[pair, ahead], yr.at[pair, way, step])

    def deliver(pair):
        for way in range(2):
            yc[pair, way, 3].wait_recv()
        done = total[pair, mine] + yr[pair, 0, 3] + yr[pair, 1, 3]
        for part in range(2):
            fs[pair, part, 0:OWN] = done[part * OWN : (part + 1) * OWN]
            fs[pair, part, OWN:PART] = done[BLOCK:ROWS]
            same = at_home & (zl == part)

            @pl.when(same)
            def _():
                fr[pair, zl] = fs[pair, part]

            @pl.when(jnp.logical_not(same))
            def _():
                final_copy(pair, part).start()

    def final_copy(pair, part):
        return pltpu.make_async_remote_copy(
            src_ref=fs.at[pair, part],
            dst_ref=fr.at[pair, zl],
            send_sem=f_send.at[pair, part],
            recv_sem=f_recv.at[pair, zl],
            device_id={"y": owner_y, "zl": part, "zh": owner_h, "core": half},
            device_id_type=MESH,
        )

    def receive(pair):
        for part in range(2):

            @pl.when(jnp.logical_not(at_home & (zl == part)))
            def _():
                pltpu.make_async_remote_copy(
                    src_ref=fs.at[pair, part],
                    dst_ref=fr.at[pair, part],
                    send_sem=f_send.at[pair, part],
                    recv_sem=f_recv.at[pair, part],
                    device_id={"y": owner_y, "zl": part, "zh": owner_h, "core": half},
                    device_id_type=MESH,
                ).wait_recv()

        out_ref[pair] = fr[pair, 0] + fr[pair, 1]

    for pair in range(PAIRS):
        z["p", pair].wait_recv()
        multiply(pair, 0, 0)
    for pair in range(PAIRS):
        pass_on(pair, 0, 0)

    z["b", 0].wait_recv()
    z["s", 0].wait_recv()
    multiply(0, 1, 0)
    forward(0)
    pass_on(0, 1, 0)
    z["ap", 0].wait_recv()
    multiply(0, 0, 1)
    multiply(0, 1, 1)
    pass_on(0, 0, 1)
    pass_on(0, 1, 1)
    collect(0, 0, 0)
    collect(1, 0, 0)
    collect(0, 1, 0)
    collect(0, 0, 1)
    collect(0, 1, 1)
    y_step(0, 0)

    z["b", 1].wait_recv()
    z["s", 1].wait_recv()
    multiply(1, 1, 0)
    y_step(0, 1)
    forward(1)
    pass_on(1, 1, 0)
    y_step(0, 2)
    z["ap", 1].wait_recv()
    multiply(1, 0, 1)
    multiply(1, 1, 1)
    y_step(0, 3)
    pass_on(1, 0, 1)
    pass_on(1, 1, 1)
    collect(1, 1, 0)
    deliver(0)
    collect(1, 0, 1)
    collect(1, 1, 1)
    for step in range(4):
        y_step(1, step)
    receive(0)
    deliver(1)
    receive(1)

    for copy in sent:
        copy.wait_send()
    for pair in range(PAIRS):
        for part in range(2):

            @pl.when(jnp.logical_not(at_home & (zl == part)))
            def _():
                final_copy(pair, part).wait_send()


def cross(x1, x2, stat):
    blocks = 4 * PAIRS
    dma = pltpu.SemaphoreType.DMA
    vmem = pl.BlockSpec(memory_space=pltpu.VMEM)
    return pl.pallas_call(
        cross_kernel,
        out_shape=jax.ShapeDtypeStruct((PAIRS, PART, WIDTH), F32),
        in_specs=[vmem, vmem, vmem],
        out_specs=vmem,
        scratch_shapes=[
            pltpu.VMEM((PAIRS, IMG_DEV, WIDTH), BF16),
            pltpu.VMEM((PAIRS, IMG_DEV, WIDTH), BF16),
            pltpu.VMEM((PAIRS, IMG_DEV, WIDTH), BF16),
            pltpu.VMEM((PAIRS, WIDTH, IMG_DEV), BF16),
            pltpu.VMEM((PAIRS, STAT, WIDTH), F32),
            pltpu.VMEM((PAIRS, 2, 2, STAT, WIDTH), F32),
            pltpu.VMEM((blocks, NX, 2, ROWS, WIDTH), F32),
            pltpu.VMEM((blocks, ROWS, WIDTH), F32),
            pltpu.VMEM((blocks, ROWS, WIDTH), F32),
            pltpu.VMEM((blocks, 2, ROWS, WIDTH), F32),
            pltpu.VMEM((blocks, 2, ROWS, WIDTH), F32),
            pltpu.VMEM((PAIRS, NY, ROWS, WIDTH), F32),
            pltpu.VMEM((PAIRS, 2, 4, ROWS, WIDTH), F32),
            pltpu.VMEM((PAIRS, 2, PART, WIDTH), F32),
            pltpu.VMEM((PAIRS, 2, PART, WIDTH), F32),
            dma((PAIRS, 5)),
            dma((PAIRS, 5)),
            dma((blocks, 6)),
            dma((blocks, 6)),
            dma((PAIRS, 2, 4)),
            dma((PAIRS, 2, 4)),
            dma((PAIRS, 2)),
            dma((PAIRS, 2)),
        ],
        compiler_params=pltpu.CompilerParams(collective_id=0, has_side_effects=True),
        name="cross",
    )(x1, x2, stat)


def local(embeddings, slot_image, slot_view, pair_table):
    summed = cross(*select(pair_table, slot_image, slot_view, embeddings))
    offset = lax.axis_index("x") * BLOCK + lax.axis_index("zl") * OWN
    products = summed[:, :OWN]
    count = summed[:, OWN + 4, 0][:, None]
    mean_first = summed[:, OWN] / count
    square_first = summed[:, OWN + 1] / count
    mean_second = lax.dynamic_slice_in_dim(summed[:, OWN + 2], offset, OWN, 1) / count
    square_second = lax.dynamic_slice_in_dim(summed[:, OWN + 3], offset, OWN, 1) / count
    spread_first = jnp.sqrt(square_first - mean_first * mean_first + EPS)
    spread_second = jnp.sqrt(square_second - mean_second * mean_second + EPS)
    block = (products / count[:, :, None] - mean_second[:, :, None] * mean_first[:, None, :]) / (
        spread_second[:, :, None] * spread_first[:, None, :]
    )
    return jnp.swapaxes(block, 1, 2)


def solution(mesh):
    split = Mesh(mesh.devices.reshape(NY, NX, 2, 4, 2), AXES)
    placed = (P(DP, FEAT), P(DP), P(DP), P())
    return jax.shard_map(local, mesh=split, in_specs=placed, out_specs=P(None, FEAT, DP), check_vma=False)
```

time: 297 us -> 106 us (0.36); the launches traced: 292 us -> 106 us
  blocking collectives: 120 us -> 0 us
  Pallas kernels: 0 us -> 102 us
  waiting for transfers between devices: 97.1 us -> 0 us
  starting transfers between devices: 20.6 us -> 0 us
  matrix products: 16.9 us -> 0 us
  other arithmetic: 18.5 us -> 2.59 us
  between operations: 14.7 us -> 0.03 us
    psum x5 -> x0, blocking collectives: 120 us -> none  [one_axis_at_a_time(): array = lax.psum(array, axis)]
    pallas_call x0 -> x2, Pallas kernels: none -> 102 us  [the longest x1 92.8 us: cross(): pl.pallas_call(cross_kernel, out_shape=jax.ShapeDtypeStruct((PAIRS, PART,...]
    all_gather x2 -> x0, waiting for transfers between devices: 97 us -> none  [local(): lax.all_gather(second_rows, FEAT, axis=1, tiled=True)]
    all_to_all x2 -> x0, starting transfers between devices: 20.4 us -> none  [summed_on_arrival(): lax.all_to_all(parts, axis, split_axis=0, concat_axis=0, tiled=True)]
    dot_general x6 -> x0, matrix products: 16.9 us -> none  [the longest x4 9.6 us: select_rows(): jnp.dot(selection, embeddings, preferred_element_type=jnp.float32)]
    reduce_sum x4 -> x0, other arithmetic: 9.73 us -> none  [the longest x1 5.65 us: select_rows(): found = jnp.sum(selection.astype(jnp.float32), axis=1) > 0.5]
    eq x1 -> x0, other arithmetic: 3.27 us -> none  [select_rows(): slot_view[None, :] == view_id]
  transfers between devices with their start and end apart: 4 -> 0, of which waited for: 2 -> 0; matrix products, arithmetic and copies ran while one was open for 6% -> 0% of each run, Pallas kernels for 0% -> 0%
where the time goes in v1:
time: 106 us
  Pallas kernels  102 us (96%)
  other arithmetic  2.59 us (2%)
    pallas_call x1, Pallas kernels, cross(): pl.pallas_call(cross_kernel, out_shape=jax.ShapeDtypeStruct((PAIRS, PART,...  92.8 us
    pallas_call x1, Pallas kernels, select(): pl.pallas_call(select_kernel, grid=(steps,), out_shape=(jax.ShapeDtypeStr...  9.27 us

profile of v1, /device:TPU:6, one launch (start us, length us, event | category | flops | bytes accessed | tf_op | source)
XLA Modules:
  0.0 105.6 jit_solution(1051328527491057249)
XLA Ops:
  0.0 9.3 %select.1 = (bf16[2,512,256]{2,1,0:T(8,128)(2,1)}, bf16[2,256,512]{2,1,0:T(8,128)(2,1)}, f32[2,8,256]{2,1,0:T(8,128)}) custom-call(s32[2,2]{1,0:T(2,128)} %pair_ref.1, s32[40,128]{1,0:T(8,128)} %bitcast.10, s32[40,128]{1,0:T(8,128)} %bitcast.11, bf16[5120,256]{1,0:T(8,128)(2,1)} %emb_ref.1), custom_call_target="tpu_custom_call" | custom-call | tf_op jit(solution)/shard_map/select/pallas_call | solution.py:74
  9.3 92.8 %cross.1 = f32[2,40,256]{2,1,0:T(8,128)} custom-call(bf16[2,512,256]{2,1,0:T(8,128)(2,1)} %get-tuple-element.8.x1_ref, bf16[2,256,512]{2,1,0:T(8,128)(2,1)} %get-tuple-element.9.x2_ref, f32[2,8,256]{2,1,0:T(8,128)} %get-tuple-element.10.stat_ref), custom_call_target="tpu_custom_call" | custom-call | tf_op jit(solution)/shard_map/cross/pallas_call | solution.py:348
  102.1 0.8 slice_reduce_fusion
  102.9 0.9 fusion
  103.8 0.1 constant_dynamic-slice_fusion
  103.9 0.1 add_sqrt_fusion.1
  104.0 1.6 %divide_bitcast_fusion = f32[2,256,32]{1,2,0:T(8,128)} fusion(f32[2,40,256]{2,1,0:T(8,128)} %cross.1, f32[2,256]{1,0:T(2,128)S(1)} %get-tuple-element.19, f32[2,32]{1,0:T(2,128)S(1)} %get-tuple-element.11, f32[2,256]{1,0:T(2,128)S(1)} %get-tuple-element.20, f32[2,32]{1,0:T(2,128)S(1)} %get-tuple-element.12, f32[2]{0:T(128)S(1)} %slice_reduce_fusion), kind=kLoop, calls=%fused_computation | loop fusion | flops 81920 | bytes 135688 | tf_op jit(solution)/shard_map/transpose | solution.py:397
  (1 shorter events, 0.0 us)

commit v2 on v1

--- a/solution.py
+++ b/solution.py
@@ -18,6 +18,8 @@
 PART = OWN + STAT
 CUT = 40
 SLOTS = 1024
+STEPS = 5
+TILE = SLOTS // 128
 VIEW_STRIDE = 16
 AXES = ("y", "x", "zl", "zh", "core")
 FEAT = ("zh", "core")
@@ -28,84 +30,15 @@
 MESH = pl.DeviceIdType.MESH
 
 
-def select_kernel(pair_ref, image_ref, view_ref, emb_ref, x1_ref, x2_ref, stat_ref, acc, found):
-    step = pl.program_id(0)
-
-    @pl.when(step == 0)
-    def _():
-        acc[...] = jnp.zeros_like(acc)
-        found[...] = jnp.zeros_like(found)
-
-    base = lax.axis_index(DP) * IMG_DEV
-    key = image_ref[...] * VIEW_STRIDE + view_ref[...]
-    wanted = (lax.broadcasted_iota(jnp.int32, (IMG_DEV, 128), 0) + base) * VIEW_STRIDE
-    for pair in range(PAIRS):
-        for side in range(2):
-            target = wanted + pair_ref[pair, side]
-            hits = [
-                jnp.where(key[row : row + 1, :] == target, 1.0, 0.0) for row in range(SLOTS // 128)
-            ]
-            chosen = jnp.concatenate([hit.astype(BF16) for hit in hits], axis=1)
-            acc[2 * pair + side] += jnp.dot(chosen, emb_ref[...], preferred_element_type=F32)
-            if side == 1:
-                found[pair] += sum(hits[1:], hits[0])
-
-    @pl.when(step == pl.num_programs(0) - 1)
-    def _():
-        row = lax.broadcasted_iota(jnp.int32, (STAT, WIDTH), 0)
-        for pair in range(PAIRS):
-            present = jnp.sum(found[pair], axis=1, keepdims=True)
-            x1_ref[pair] = jnp.where(present > 0.5, acc[2 * pair], 0.0).astype(BF16)
-            second = acc[2 * pair + 1]
-            x2_ref[pair] = second.T.astype(BF16)
-            total = jnp.sum(second, axis=0, keepdims=True)
-            square = jnp.sum(second * second, axis=0, keepdims=True)
-            count = jnp.sum(present)
-            stat_ref[pair] = jnp.where(
-                row == 2, total, jnp.where(row == 3, square, jnp.where(row == 4, count, 0.0))
-            )
-
-
-def select(pair_table, slot_image, slot_view, embeddings):
-    slots = embeddings.shape[0]
-    steps = slots // SLOTS
-    ids = pl.BlockSpec((SLOTS // 128, 128), lambda k: (k, 0))
-    whole = lambda *shape: pl.BlockSpec(shape, lambda k: (0,) * len(shape))
-    return pl.pallas_call(
-        select_kernel,
-        grid=(steps,),
-        out_shape=(
-            jax.ShapeDtypeStruct((PAIRS, IMG_DEV, WIDTH), BF16),
-            jax.ShapeDtypeStruct((PAIRS, WIDTH, IMG_DEV), BF16),
-            jax.ShapeDtypeStruct((PAIRS, STAT, WIDTH), F32),
-        ),
-        in_specs=[
-            pl.BlockSpec(memory_space=pltpu.SMEM),
-            ids,
-            ids,
-            pl.BlockSpec((SLOTS, WIDTH), lambda k: (k, 0)),
-        ],
-        out_specs=(
-            whole(PAIRS, IMG_DEV, WIDTH),
-            whole(PAIRS, WIDTH, IMG_DEV),
-            whole(PAIRS, STAT, WIDTH),
-        ),
-        scratch_shapes=[
-            pltpu.VMEM((2 * PAIRS, IMG_DEV, WIDTH), F32),
-            pltpu.VMEM((PAIRS, IMG_DEV, 128), F32),
-        ],
-        name="select",
-    )(pair_table, slot_image.reshape(slots // 128, 128), slot_view.reshape(slots // 128, 128), embeddings)
-
-
 def shift_of(plane, core):
     return 7 + core + 4 * (plane // 2)
 
 
 def cross_kernel(
-    x1_ref, x2_ref, stat_ref, out_ref,
+    pair_ref, image_ref, view_ref, emb_ref, out_ref,
+    emb, acc, found, x1_ref, x2_ref, stat_ref,
     x1p, x1a, x1ap, x2b, statb, x1stat, cb, relay_p, relay_m, from_m, from_p, total, yr, fs, fr,
-    z_send, z_recv, x_send, x_recv, y_send, y_recv, f_send, f_recv,
+    emb_sem, z_send, z_recv, x_send, x_recv, y_send, y_recv, f_send, f_recv,
 ):
     y, x, zl, h, core = [lax.axis_index(axis) for axis in AXES]
     plane_a = h + 1 - 2 * (h % 2)
@@ -125,6 +58,12 @@
     src_ih = (src_h + h) % 2
     src_y = (4 * src_jb + 2 * src_ih + core + shift_of(src_h, src_core)) % NY
 
+    loads = []
+    for step in range(STEPS):
+        rows = slice(step * SLOTS, (step + 1) * SLOTS)
+        loads.append(pltpu.make_async_copy(emb_ref.at[rows], emb.at[rows], emb_sem.at[step]))
+        loads[-1].start()
+
     barrier = pltpu.get_barrier_semaphore()
     for peer in ({"x": xp}, {"x": xm}, {"y": yp}, {"y": ym}, {"zh": plane_a}, {"zh": plane_b}, {"core": other}):
         pl.semaphore_signal(barrier, inc=1, device_id=peer, device_id_type=MESH)
@@ -139,8 +78,6 @@
                 device_id_type=MESH,
             )
 
-    pl.semaphore_wait(barrier, 9 - at_home.astype(jnp.int32))
-
     sent = []
 
     def send(src, dst, send_sem, recv_sem, peer):
@@ -152,19 +89,61 @@
         return copy
 
     z = {}
-    for pair in range(PAIRS):
-        for slot, (name, src, dst, peer) in enumerate(
-            (
-                ("p", x1_ref, x1p, {"core": other}),
-                ("b", x2_ref, x2b, {"zh": plane_b}),
-                ("s", stat_ref, statb, {"zh": plane_b}),
-                ("a", x1_ref, x1a, {"zh": plane_a}),
-            )
-        ):
-            z[name, pair] = send(src.at[pair], dst.at[pair], z_send.at[pair, slot], z_recv.at[pair, slot], peer)
+
+    def offer(pair, name):
+        slot, src, dst, peer = {
+            "p": (0, x1_ref, x1p, {"core": other}),
+            "b": (1, x2_ref, x2b, {"zh": plane_b}),
+            "s": (2, stat_ref, statb, {"zh": plane_b}),
+            "a": (3, x1_ref, x1a, {"zh": plane_a}),
+        }[name]
+        z[name, pair] = send(src.at[pair], dst.at[pair], z_send.at[pair, slot], z_recv.at[pair, slot], peer)
+
+    def arrive(pair, *names):
+        for name in names:
+            z[name, pair].wait_recv()
+
+    base = (y * NX * 2 + x * 2 + zl) * IMG_DEV
+    wanted = (lax.broadcasted_iota(jnp.int32, (IMG_DEV, 128), 0) + base) * VIEW_STRIDE
+
+    def pick(pair, side):
+        target = wanted + pair_ref[pair, side]
+        acc[...] = jnp.zeros_like(acc)
+        if side:
+            found[pair] = jnp.zeros_like(found[pair])
+
+        def step(index, carry):
+            key = image_ref[pl.ds(pl.multiple_of(index * TILE, TILE), TILE), :] * VIEW_STRIDE
+            key += view_ref[pl.ds(pl.multiple_of(index * TILE, TILE), TILE), :]
+            hits = [jnp.where(key[row : row + 1, :] == target, 1.0, 0.0) for row in range(TILE)]
+            chosen = jnp.concatenate([hit.astype(BF16) for hit in hits], axis=1)
+            rows = emb[pl.ds(pl.multiple_of(index * SLOTS, SLOTS), SLOTS), :]
+            acc[...] += jnp.dot(chosen, rows, preferred_element_type=F32)
+            if side:
+                found[pair] += sum(hits[1:], hits[0])
+            return carry
+
+        lax.fori_loop(0, STEPS, step, 0)
+
+    def pick_second(pair):
+        pick(pair, 1)
+        row = lax.broadcasted_iota(jnp.int32, (STAT, WIDTH), 0)
+        second = acc[...]
+        x2_ref[pair] = second.T.astype(BF16)
+        plain = jnp.sum(second, axis=0, keepdims=True)
+        square = jnp.sum(second * second, axis=0, keepdims=True)
+        count = jnp.sum(found[pair])
+        stat_ref[pair] = jnp.where(
+            row == 2, plain, jnp.where(row == 3, square, jnp.where(row == 4, count, 0.0))
+        )
+
+    def pick_first(pair):
+        pick(pair, 0)
+        present = jnp.sum(found[pair], axis=1, keepdims=True)
+        x1_ref[pair] = jnp.where(present > 0.5, acc[...], 0.0).astype(BF16)
 
     def forward(pair):
-        z["a", pair].wait_recv()
+        arrive(pair, "a")
         z["ap", pair] = send(
             x1a.at[pair], x1ap.at[pair], z_send.at[pair, 4], z_recv.at[pair, 4], {"core": other}
         )
@@ -283,20 +262,49 @@
                     device_id_type=MESH,
                 ).wait_recv()
 
-        out_ref[pair] = fr[pair, 0] + fr[pair, 1]
-
-    for pair in range(PAIRS):
-        z["p", pair].wait_recv()
-        multiply(pair, 0, 0)
-    for pair in range(PAIRS):
-        pass_on(pair, 0, 0)
-
-    z["b", 0].wait_recv()
-    z["s", 0].wait_recv()
+        both = fr[pair, 0] + fr[pair, 1]
+        count = both[OWN + 4 : OWN + 5, 0:1]
+        lane = lax.broadcasted_iota(jnp.int32, (OWN, WIDTH), 1)
+        row = lax.broadcasted_iota(jnp.int32, (OWN, WIDTH), 0)
+        own = lane == row + (x * BLOCK + zl * OWN)
+
+        def column(line):
+            return jnp.sum(jnp.where(own, line, 0.0), axis=1, keepdims=True)
+
+        mean_first = both[OWN : OWN + 1] / count
+        square_first = both[OWN + 1 : OWN + 2] / count
+        mean_second = column(both[OWN + 2 : OWN + 3]) / count
+        square_second = column(both[OWN + 3 : OWN + 4]) / count
+        spread_first = jnp.sqrt(square_first - mean_first * mean_first + EPS)
+        spread_second = jnp.sqrt(square_second - mean_second * mean_second + EPS)
+        out_ref[pair] = (both[0:OWN] / count - mean_second * mean_first) / (spread_second * spread_first)
+
+    for load in loads:
+        load.wait()
+    pick_second(0)
+    pl.semaphore_wait(barrier, 9 - at_home.astype(jnp.int32))
+    offer(0, "b")
+    offer(0, "s")
+    pick_first(0)
+    offer(0, "a")
+    offer(0, "p")
+    pick_second(1)
+    offer(1, "b")
+    offer(1, "s")
+    arrive(0, "p")
+    multiply(0, 0, 0)
+    pick_first(1)
+    offer(1, "a")
+    offer(1, "p")
+    pass_on(0, 0, 0)
+    arrive(1, "p")
+    multiply(1, 0, 0)
+    arrive(0, "b", "s")
     multiply(0, 1, 0)
+    pass_on(1, 0, 0)
     forward(0)
     pass_on(0, 1, 0)
-    z["ap", 0].wait_recv()
+    arrive(0, "ap")
     multiply(0, 0, 1)
     multiply(0, 1, 1)
     pass_on(0, 0, 1)
@@ -304,30 +312,30 @@
     collect(0, 0, 0)
     collect(1, 0, 0)
     collect(0, 1, 0)
+    arrive(1, "b", "s")
+    multiply(1, 1, 0)
+    forward(1)
     collect(0, 0, 1)
+    arrive(1, "ap")
+    multiply(1, 0, 1)
+    multiply(1, 1, 1)
+    pass_on(1, 1, 0)
     collect(0, 1, 1)
     y_step(0, 0)
-
-    z["b", 1].wait_recv()
-    z["s", 1].wait_recv()
-    multiply(1, 1, 0)
+    pass_on(1, 0, 1)
     y_step(0, 1)
-    forward(1)
-    pass_on(1, 1, 0)
+    pass_on(1, 1, 1)
     y_step(0, 2)
-    z["ap", 1].wait_recv()
-    multiply(1, 0, 1)
-    multiply(1, 1, 1)
+    collect(1, 1, 0)
     y_step(0, 3)
-    pass_on(1, 0, 1)
-    pass_on(1, 1, 1)
-    collect(1, 1, 0)
+    collect(1, 0, 1)
     deliver(0)
-    collect(1, 0, 1)
     collect(1, 1, 1)
-    for step in range(4):
-        y_step(1, step)
+    y_step(1, 0)
+    y_step(1, 1)
     receive(0)
+    y_step(1, 2)
+    y_step(1, 3)
     deliver(1)
     receive(1)
 
@@ -341,16 +349,22 @@
                 final_copy(pair, part).wait_send()
 
 
-def cross(x1, x2, stat):
+def cross(pair_table, image, view, embeddings):
     blocks = 4 * PAIRS
     dma = pltpu.SemaphoreType.DMA
     vmem = pl.BlockSpec(memory_space=pltpu.VMEM)
     return pl.pallas_call(
         cross_kernel,
-        out_shape=jax.ShapeDtypeStruct((PAIRS, PART, WIDTH), F32),
-        in_specs=[vmem, vmem, vmem],
+        out_shape=jax.ShapeDtypeStruct((PAIRS, OWN, WIDTH), F32),
+        in_specs=[pl.BlockSpec(memory_space=pltpu.SMEM), vmem, vmem, pl.BlockSpec(memory_space=pl.ANY)],
         out_specs=vmem,
         scratch_shapes=[
+            pltpu.VMEM((STEPS * SLOTS, WIDTH), BF16),
+            pltpu.VMEM((IMG_DEV, WIDTH), F32),
+            pltpu.VMEM((PAIRS, IMG_DEV, 128), F32),
+            pltpu.VMEM((PAIRS, IMG_DEV, WIDTH), BF16),
+            pltpu.VMEM((PAIRS, WIDTH, IMG_DEV), BF16),
+            pltpu.VMEM((PAIRS, STAT, WIDTH), F32),
             pltpu.VMEM((PAIRS, IMG_DEV, WIDTH), BF16),
             pltpu.VMEM((PAIRS, IMG_DEV, WIDTH), BF16),
             pltpu.VMEM((PAIRS, IMG_DEV, WIDTH), BF16),
@@ -366,6 +380,7 @@
             pltpu.VMEM((PAIRS, 2, 4, ROWS, WIDTH), F32),
             pltpu.VMEM((PAIRS, 2, PART, WIDTH), F32),
             pltpu.VMEM((PAIRS, 2, PART, WIDTH), F32),
+            dma((STEPS,)),
             dma((PAIRS, 5)),
             dma((PAIRS, 5)),
             dma((blocks, 6)),
@@ -377,23 +392,12 @@
         ],
         compiler_params=pltpu.CompilerParams(collective_id=0, has_side_effects=True),
         name="cross",
-    )(x1, x2, stat)
+    )(pair_table, image, view, embeddings)
 
 
 def local(embeddings, slot_image, slot_view, pair_table):
-    summed = cross(*select(pair_table, slot_image, slot_view, embeddings))
-    offset = lax.axis_index("x") * BLOCK + lax.axis_index("zl") * OWN
-    products = summed[:, :OWN]
-    count = summed[:, OWN + 4, 0][:, None]
-    mean_first = summed[:, OWN] / count
-    square_first = summed[:, OWN + 1] / count
-    mean_second = lax.dynamic_slice_in_dim(summed[:, OWN + 2], offset, OWN, 1) / count
-    square_second = lax.dynamic_slice_in_dim(summed[:, OWN + 3], offset, OWN, 1) / count
-    spread_first = jnp.sqrt(square_first - mean_first * mean_first + EPS)
-    spread_second = jnp.sqrt(square_second - mean_second * mean_second + EPS)
-    block = (products / count[:, :, None] - mean_second[:, :, None] * mean_first[:, None, :]) / (
-        spread_second[:, :, None] * spread_first[:, None, :]
-    )
+    shape = (STEPS * TILE, 128)
+    block = cross(pair_table, slot_image.reshape(shape), slot_view.reshape(shape), embeddings)
     return jnp.swapaxes(block, 1, 2)
 
 

time: 106 us -> 96.5 us (0.910)
  Pallas kernels: 102 us -> 94.4 us
  other arithmetic: 2.59 us -> 0 us
    pallas_call x2 -> x1, Pallas kernels: 102 us -> 94.4 us  [cross(): pl.pallas_call(cross_kernel, out_shape=jax.ShapeDtypeStruct((PAIRS, OWN,...]
    transpose x1 -> x0, other arithmetic: 1.57 us -> none  [local(): return jnp.swapaxes(block, 1, 2)]
    unnamed x1, local copies, waits for them, and re-layouts: 0.01 us -> 1.47 us
where the time goes in v2:
time: 96.5 us; the launch traced here: 95.9 us
  Pallas kernels  94.4 us (98%)
  local copies, waits for them, and re-layouts  1.47 us (2%)
    pallas_call x1, Pallas kernels, cross(): pl.pallas_call(cross_kernel, out_shape=jax.ShapeDtypeStruct((PAIRS, OWN,...  94.4 us

profile of v2, /device:TPU:6, one launch (start us, length us, event | category | flops | bytes accessed | tf_op | source)
XLA Modules:
  0.0 95.9 jit_solution(14443801592690021518)
XLA Ops:
  0.0 94.4 %cross.1 = f32[2,32,256]{2,1,0:T(8,128)} custom-call(s32[2,2]{1,0:T(2,128)} %pair_ref.1, s32[40,128]{1,0:T(8,128)} %bitcast.4, s32[40,128]{1,0:T(8,128)} %bitcast.5, bf16[5120,256]{1,0:T(8,128)(2,1)} %emb_ref.1), custom_call_target="tpu_custom_call" | custom-call | tf_op jit(solution)/shard_map/cross/pallas_call | solution.py:356
  94.4 1.5 %copy.6 = f32[2,256,32]{1,2,0:T(8,128)} copy(f32[2,256,32]{1,2,0:T(8,128)} %bitcast.3) | data formatting | bytes 131072

commit v3 on v2

--- a/solution.py
+++ b/solution.py
@@ -14,9 +14,17 @@
 NX, NY = 4, 8
 BLOCK = 64
 STAT = 8
-ROWS = BLOCK + STAT
+LEAD = 40
+REST = BLOCK - LEAD
+ROWS = LEAD + STAT
 PART = OWN + STAT
-CUT = 40
+CUT = 24
+REST_CUT = 16
+GROUPS = (
+    ((0, 0, 0), (1, 0, 0)),
+    ((0, 1, 0), (0, 0, 1), (0, 1, 1)),
+    ((1, 1, 0), (1, 0, 1), (1, 1, 1)),
+)
 SLOTS = 1024
 STEPS = 5
 TILE = SLOTS // 128
@@ -36,9 +44,10 @@
 
 def cross_kernel(
     pair_ref, image_ref, view_ref, emb_ref, out_ref,
-    emb, acc, found, x1_ref, x2_ref, stat_ref,
+    emb, acc, found, counts, x1_ref, x2_ref, stat_ref,
     x1p, x1a, x1ap, x2b, statb, x1stat, cb, relay_p, relay_m, from_m, from_p, total, yr, fs, fr,
-    emb_sem, z_send, z_recv, x_send, x_recv, y_send, y_recv, f_send, f_recv,
+    w0, w1, w2, v0, v1, v2, rest, rest_in,
+    emb_sem, z_send, z_recv, x_send, x_recv, y_send, y_recv, f_send, f_recv, w_send, w_recv, r_send, r_recv,
 ):
     y, x, zl, h, core = [lax.axis_index(axis) for axis in AXES]
     plane_a = h + 1 - 2 * (h % 2)
@@ -57,6 +66,8 @@
     src_h = jh + src_jb * (3 - 2 * jh)
     src_ih = (src_h + h) % 2
     src_y = (4 * src_jb + 2 * src_ih + core + shift_of(src_h, src_core)) % NY
+    rest_y = 2 * x + core
+    rest_home = (rest_y == y) & (src_h == h) & (zl == 1)
 
     loads = []
     for step in range(STEPS):
@@ -78,6 +89,18 @@
                 device_id_type=MESH,
             )
 
+    for from_x in range(NX):
+        for part in range(2):
+
+            @pl.when((zl == 1) & jnp.logical_not(rest_home & (x == from_x) & (zl == part)))
+            def _():
+                pl.semaphore_signal(
+                    barrier,
+                    inc=1,
+                    device_id={"y": rest_y, "x": from_x, "zl": part, "zh": src_h, "core": src_core},
+                    device_id_type=MESH,
+                )
+
     sent = []
 
     def send(src, dst, send_sem, recv_sem, peer):
@@ -108,39 +131,41 @@
 
     def pick(pair, side):
         target = wanted + pair_ref[pair, side]
+        second = wanted + pair_ref[pair, 1]
         acc[...] = jnp.zeros_like(acc)
-        if side:
-            found[pair] = jnp.zeros_like(found[pair])
+        if side == 0:
+            found[...] = jnp.zeros_like(found)
 
         def step(index, carry):
             key = image_ref[pl.ds(pl.multiple_of(index * TILE, TILE), TILE), :] * VIEW_STRIDE
             key += view_ref[pl.ds(pl.multiple_of(index * TILE, TILE), TILE), :]
-            hits = [jnp.where(key[row : row + 1, :] == target, 1.0, 0.0) for row in range(TILE)]
-            chosen = jnp.concatenate([hit.astype(BF16) for hit in hits], axis=1)
+            keys = [key[row : row + 1, :] for row in range(TILE)]
+            chosen = jnp.concatenate([jnp.where(one == target, 1.0, 0.0).astype(BF16) for one in keys], axis=1)
             rows = emb[pl.ds(pl.multiple_of(index * SLOTS, SLOTS), SLOTS), :]
             acc[...] += jnp.dot(chosen, rows, preferred_element_type=F32)
-            if side:
-                found[pair] += sum(hits[1:], hits[0])
+            if side == 0:
+                hits = [jnp.where(one == second, 1.0, 0.0) for one in keys]
+                found[...] += sum(hits[1:], hits[0])
             return carry
 
         lax.fori_loop(0, STEPS, step, 0)
+
+    def pick_first(pair):
+        pick(pair, 0)
+        present = jnp.sum(found[...], axis=1, keepdims=True)
+        x1_ref[pair] = jnp.where(present > 0.5, acc[...], 0.0).astype(BF16)
+        counts[pair] = jnp.broadcast_to(jnp.sum(present, axis=0, keepdims=True), (1, WIDTH))
 
     def pick_second(pair):
         pick(pair, 1)
         row = lax.broadcasted_iota(jnp.int32, (STAT, WIDTH), 0)
-        second = acc[...]
-        x2_ref[pair] = second.T.astype(BF16)
-        plain = jnp.sum(second, axis=0, keepdims=True)
-        square = jnp.sum(second * second, axis=0, keepdims=True)
-        count = jnp.sum(found[pair])
+        rows = acc[...]
+        x2_ref[pair] = rows.T.astype(BF16)
+        plain = jnp.sum(rows, axis=0, keepdims=True)
+        square = jnp.sum(rows * rows, axis=0, keepdims=True)
         stat_ref[pair] = jnp.where(
-            row == 2, plain, jnp.where(row == 3, square, jnp.where(row == 4, count, 0.0))
-        )
-
-    def pick_first(pair):
-        pick(pair, 0)
-        present = jnp.sum(found[pair], axis=1, keepdims=True)
-        x1_ref[pair] = jnp.where(present > 0.5, acc[...], 0.0).astype(BF16)
+            row == 2, plain, jnp.where(row == 3, square, jnp.where(row == 4, counts[pair], 0.0))
+        )
 
     def forward(pair):
         arrive(pair, "a")
@@ -156,6 +181,9 @@
 
     def multiply(pair, jb, ih):
         k = block_of(pair, jb, ih)
+        group, place = next(
+            (g, blocks.index((pair, jb, ih))) for g, blocks in enumerate(GROUPS) if (pair, jb, ih) in blocks
+        )
         second = (x2b if jb else x2_ref)[pair]
         stat = (statb if jb else stat_ref)[pair]
         row = lax.broadcasted_iota(jnp.int32, (STAT, WIDTH), 0)
@@ -170,8 +198,9 @@
             product = jnp.dot(second, first, preferred_element_type=F32)
             sums = x1stat[pair, ih, slot] + stat
             for dest in range(NX):
-                cb[k, dest, half, 0:BLOCK] = product[dest * BLOCK : (dest + 1) * BLOCK]
-                cb[k, dest, half, BLOCK:ROWS] = sums
+                cb[k, dest, half, 0:LEAD] = product[dest * BLOCK : dest * BLOCK + LEAD]
+                cb[k, dest, half, LEAD:ROWS] = sums
+                w[group][2 * dest + half, place] = product[dest * BLOCK + LEAD : (dest + 1) * BLOCK]
         for slot, (src, dst, to) in enumerate(
             (
                 (cb.at[k, xa, 0], relay_p.at[k], xp),
@@ -221,13 +250,97 @@
                 total[pair, ahead] += yr[pair, way, step - 1]
             y_send_part(pair, way, step, total.at[pair, ahead], yr.at[pair, way, step])
 
+    w, v = (w0, w1, w2), (v0, v1, v2)
+    wc = {}
+
+    def w_step(group, step):
+        for way in range(2):
+            ahead = (y + (4 + step if way else 4 - step)) % NY
+            rows = slice(REST_CUT, REST) if way else slice(0, REST_CUT)
+            size = REST - REST_CUT if way else REST_CUT
+            sems = (w_send.at[group, way, step], w_recv.at[group, way, step], {"y": ym if way else yp})
+            if step == 0:
+                wc[group, way, 0] = send(
+                    w[group].at[ahead, :, rows], v[group].at[way, 0, :, 0:size], *sems
+                )
+                continue
+            wc[group, way, step - 1].wait_recv()
+            if step == 1:
+                w[group][ahead, :, rows] += v[group][way, 0, :, 0:size]
+            else:
+                w[group][ahead] += v[group][way, step - 1]
+            wc[group, way, step] = send(w[group].at[ahead], v[group].at[way, step], *sems)
+
+    def rest_copy(pair, jb, ih):
+        k = block_of(pair, jb, ih)
+        return pltpu.make_async_remote_copy(
+            src_ref=rest.at[k],
+            dst_ref=rest_in.at[pair, x, zl],
+            send_sem=r_send.at[k],
+            recv_sem=r_recv.at[pair, x, zl],
+            device_id={
+                "y": 2 * (plane_b if jb else h) + core,
+                "x": y // 2,
+                "zl": 1,
+                "zh": plane_a if ih else h,
+                "core": y % 2,
+            },
+            device_id_type=MESH,
+        )
+
+    def w_deliver(group):
+        for way in range(2):
+            wc[group, way, 3].wait_recv()
+        for place, (pair, jb, ih) in enumerate(GROUPS[group]):
+            k = block_of(pair, jb, ih)
+            rest[k] = w[group][y, place] + v[group][0, 3, place] + v[group][1, 3, place]
+            if ih:
+                rest_copy(pair, jb, ih).start()
+                continue
+            same = rest_home & (src_jb == jb)
+
+            @pl.when(same)
+            def _():
+                rest_in[pair, x, zl] = rest[k]
+
+            @pl.when(jnp.logical_not(same))
+            def _():
+                rest_copy(pair, jb, ih).start()
+
+    def rest_receive(pair):
+        @pl.when(zl == 1)
+        def _():
+            for from_x in range(NX):
+                for part in range(2):
+
+                    @pl.when(jnp.logical_not(rest_home & (x == from_x) & (zl == part)))
+                    def _():
+                        pltpu.make_async_remote_copy(
+                            src_ref=rest.at[0],
+                            dst_ref=rest_in.at[pair, from_x, part],
+                            send_sem=r_send.at[0],
+                            recv_sem=r_recv.at[pair, from_x, part],
+                            device_id={"x": xp},
+                            device_id_type=MESH,
+                        ).wait_recv()
+
+            lead = OWN - REST
+            summed = rest_in[pair, 0, 0]
+            for slot in range(1, 2 * NX):
+                summed += rest_in[pair, slot // 2, slot % 2]
+            fr[pair, 0, lead:OWN] += summed
+
     def deliver(pair):
         for way in range(2):
             yc[pair, way, 3].wait_recv()
         done = total[pair, mine] + yr[pair, 0, 3] + yr[pair, 1, 3]
         for part in range(2):
-            fs[pair, part, 0:OWN] = done[part * OWN : (part + 1) * OWN]
-            fs[pair, part, OWN:PART] = done[BLOCK:ROWS]
+            if part:
+                fs[pair, 1, 0 : LEAD - OWN] = done[OWN:LEAD]
+                fs[pair, 1, LEAD - OWN : OWN] = jnp.zeros((REST, WIDTH), F32)
+            else:
+                fs[pair, 0, 0:OWN] = done[0:OWN]
+            fs[pair, part, OWN:PART] = done[LEAD:ROWS]
             same = at_home & (zl == part)
 
             @pl.when(same)
@@ -262,6 +375,7 @@
                     device_id_type=MESH,
                 ).wait_recv()
 
+        rest_receive(pair)
         both = fr[pair, 0] + fr[pair, 1]
         count = both[OWN + 4 : OWN + 5, 0:1]
         lane = lax.broadcasted_iota(jnp.int32, (OWN, WIDTH), 1)
@@ -281,62 +395,77 @@
 
     for load in loads:
         load.wait()
+    pick_first(0)
+    pl.semaphore_wait(barrier, 13 - at_home.astype(jnp.int32) - rest_home.astype(jnp.int32))
+    offer(0, "a")
+    offer(0, "p")
     pick_second(0)
-    pl.semaphore_wait(barrier, 9 - at_home.astype(jnp.int32))
     offer(0, "b")
     offer(0, "s")
-    pick_first(0)
-    offer(0, "a")
-    offer(0, "p")
-    pick_second(1)
-    offer(1, "b")
-    offer(1, "s")
     arrive(0, "p")
     multiply(0, 0, 0)
     pick_first(1)
     offer(1, "a")
     offer(1, "p")
     pass_on(0, 0, 0)
+    pick_second(1)
+    offer(1, "b")
+    offer(1, "s")
     arrive(1, "p")
     multiply(1, 0, 0)
+    w_step(0, 0)
+    forward(0)
+    pass_on(1, 0, 0)
+    w_step(0, 1)
     arrive(0, "b", "s")
     multiply(0, 1, 0)
-    pass_on(1, 0, 0)
-    forward(0)
-    pass_on(0, 1, 0)
+    w_step(0, 2)
     arrive(0, "ap")
     multiply(0, 0, 1)
     multiply(0, 1, 1)
+    w_step(1, 0)
+    pass_on(0, 1, 0)
+    w_step(0, 3)
     pass_on(0, 0, 1)
     pass_on(0, 1, 1)
+    w_step(1, 1)
     collect(0, 0, 0)
     collect(1, 0, 0)
+    w_deliver(0)
+    forward(1)
     collect(0, 1, 0)
+    w_step(1, 2)
     arrive(1, "b", "s")
     multiply(1, 1, 0)
-    forward(1)
     collect(0, 0, 1)
     arrive(1, "ap")
     multiply(1, 0, 1)
     multiply(1, 1, 1)
+    w_step(2, 0)
     pass_on(1, 1, 0)
     collect(0, 1, 1)
     y_step(0, 0)
+    w_step(1, 3)
     pass_on(1, 0, 1)
+    pass_on(1, 1, 1)
+    w_step(2, 1)
     y_step(0, 1)
-    pass_on(1, 1, 1)
-    y_step(0, 2)
+    w_deliver(1)
     collect(1, 1, 0)
-    y_step(0, 3)
     collect(1, 0, 1)
-    deliver(0)
     collect(1, 1, 1)
     y_step(1, 0)
+    w_step(2, 2)
+    y_step(0, 2)
     y_step(1, 1)
-    receive(0)
+    w_step(2, 3)
+    y_step(0, 3)
     y_step(1, 2)
+    w_deliver(2)
+    deliver(0)
     y_step(1, 3)
     deliver(1)
+    receive(0)
     receive(1)
 
     for copy in sent:
@@ -347,6 +476,12 @@
             @pl.when(jnp.logical_not(at_home & (zl == part)))
             def _():
                 final_copy(pair, part).wait_send()
+    for group in GROUPS:
+        for pair, jb, ih in group:
+
+            @pl.when(jnp.logical_not(rest_home & (src_jb == jb) & (ih == 0)))
+            def _():
+                rest_copy(pair, jb, ih).wait_send()
 
 
 def cross(pair_table, image, view, embeddings):
@@ -361,7 +496,8 @@
         scratch_shapes=[
             pltpu.VMEM((STEPS * SLOTS, WIDTH), BF16),
             pltpu.VMEM((IMG_DEV, WIDTH), F32),
-            pltpu.VMEM((PAIRS, IMG_DEV, 128), F32),
+            pltpu.VMEM((IMG_DEV, 128), F32),
+            pltpu.VMEM((PAIRS, 1, WIDTH), F32),
             pltpu.VMEM((PAIRS, IMG_DEV, WIDTH), BF16),
             pltpu.VMEM((PAIRS, WIDTH, IMG_DEV), BF16),
             pltpu.VMEM((PAIRS, STAT, WIDTH), F32),
@@ -380,6 +516,10 @@
             pltpu.VMEM((PAIRS, 2, 4, ROWS, WIDTH), F32),
             pltpu.VMEM((PAIRS, 2, PART, WIDTH), F32),
             pltpu.VMEM((PAIRS, 2, PART, WIDTH), F32),
+            *(pltpu.VMEM((NY, len(blocks_of), REST, WIDTH), F32) for blocks_of in GROUPS),
+            *(pltpu.VMEM((2, 4, len(blocks_of), REST, WIDTH), F32) for blocks_of in GROUPS),
+            pltpu.VMEM((blocks, REST, WIDTH), F32),
+            pltpu.VMEM((PAIRS, NX, 2, REST, WIDTH), F32),
             dma((STEPS,)),
             dma((PAIRS, 5)),
             dma((PAIRS, 5)),
@@ -389,6 +529,10 @@
             dma((PAIRS, 2, 4)),
             dma((PAIRS, 2)),
             dma((PAIRS, 2)),
+            dma((len(GROUPS), 2, 4)),
+            dma((len(GROUPS), 2, 4)),
+            dma((blocks,)),
+            dma((PAIRS, NX, 2)),
         ],
         compiler_params=pltpu.CompilerParams(collective_id=0, has_side_effects=True),
         name="cross",

time: 96.5 us -> 93.3 us (0.967)
  Pallas kernels: 94.4 us -> 91.5 us
    pallas_call x1, Pallas kernels: 94.4 us -> 91.5 us  [cross(): pl.pallas_call(cross_kernel, out_shape=jax.ShapeDtypeStruct((PAIRS, OWN,...]
where the time goes in v3:
time: 93.3 us; the launch traced here: 93 us
  Pallas kernels  91.5 us (98%)
  local copies, waits for them, and re-layouts  1.47 us (2%)
    pallas_call x1, Pallas kernels, cross(): pl.pallas_call(cross_kernel, out_shape=jax.ShapeDtypeStruct((PAIRS, OWN,...  91.5 us

profile of v3, /device:TPU:6, one launch (start us, length us, event | category | flops | bytes accessed | tf_op | source)
XLA Modules:
  0.0 93.0 jit_solution(1989242042742715242)
XLA Ops:
  0.0 91.5 %cross.1 = f32[2,32,256]{2,1,0:T(8,128)} custom-call(s32[2,2]{1,0:T(2,128)} %pair_ref.1, s32[40,128]{1,0:T(8,128)} %bitcast.4, s32[40,128]{1,0:T(8,128)} %bitcast.5, bf16[5120,256]{1,0:T(8,128)(2,1)} %emb_ref.1), custom_call_target="tpu_custom_call" | custom-call | tf_op jit(solution)/shard_map/cross/pallas_call | solution.py:491
  91.5 1.5 %copy.6 = f32[2,256,32]{1,2,0:T(8,128)} copy(f32[2,256,32]{1,2,0:T(8,128)} %bitcast.3) | data formatting | bytes 131072

commit v4 on v3

--- a/solution.py
+++ b/solution.py
@@ -38,8 +38,9 @@
 MESH = pl.DeviceIdType.MESH
 
 
-def shift_of(plane, core):
-    return 7 + core + 4 * (plane // 2)
+def place_of(plane, core, jb, ih, half):
+    ahead = (1 - jb) * (ih * half + (1 - ih) * (7 - 5 * half)) + jb * (4 + 2 * ih - half)
+    return (2 * plane + core + NY + (1 - 2 * (plane % 2)) * ahead) % NY
 
 
 def cross_kernel(
@@ -55,9 +56,12 @@
     other = 1 - core
     xp, xa, xm = (x + 1) % NX, (x + 2) % NX, (x + 3) % NX
     yp, ym = (y + 1) % NY, (y + NY - 1) % NY
-    mine = (y + 2 * NY - shift_of(h, core)) % NY
-
-    jb, ih, half = mine // 4, (mine // 2) % 2, mine % 2
+    yp2, ym2 = (y + 2) % NY, (y + NY - 2) % NY
+
+    mine = (2 * NY + (1 - 2 * (h % 2)) * (y - 2 * h - core)) % NY
+    jb = ((mine + 1) // 4) % 2
+    ih = ((mine < 2) | ((mine > 4) & (mine < 7))).astype(jnp.int32)
+    half = (((mine > 0) & (mine < 4)) | (mine == 5)).astype(jnp.int32)
     owner_y = 2 * (h + jb * (3 - 2 * h)) + core
     owner_h = h + ih * (1 - 2 * (h % 2))
     at_home = (owner_y == y) & (owner_h == h) & (half == core)
@@ -65,7 +69,7 @@
     src_jb = (jh // 2 + h // 2) % 2
     src_h = jh + src_jb * (3 - 2 * jh)
     src_ih = (src_h + h) % 2
-    src_y = (4 * src_jb + 2 * src_ih + core + shift_of(src_h, src_core)) % NY
+    src_y = place_of(src_h, src_core, src_jb, src_ih, core)
     rest_y = 2 * x + core
     rest_home = (rest_y == y) & (src_h == h) & (zl == 1)
 
@@ -76,7 +80,7 @@
         loads[-1].start()
 
     barrier = pltpu.get_barrier_semaphore()
-    for peer in ({"x": xp}, {"x": xm}, {"y": yp}, {"y": ym}, {"zh": plane_a}, {"zh": plane_b}, {"core": other}):
+    for peer in ({"x": xp}, {"x": xm}, {"y": yp}, {"y": ym}, {"y": yp2}, {"y": ym2}, {"zh": plane_a}, {"zh": plane_b}, {"core": other}):
         pl.semaphore_signal(barrier, inc=1, device_id=peer, device_id_type=MESH)
     for part in range(2):
 
@@ -225,51 +229,61 @@
         for slot in (2, 3, 4, 5):
             xc[k, slot].wait_recv()
         for half in range(2):
-            total[pair, 4 * jb + 2 * ih + half] = cb[k, x, half] + from_m[k, half] + from_p[k, half]
+            total[pair, place_of(h, core, jb, ih, half)] = cb[k, x, half] + from_m[k, half] + from_p[k, half]
+
+    def y_ways(key, copies, part, landing, send_sem, recv_sem, cut, step):
+        for way in range(2):
+            one, two = (ym, ym2) if way else (yp, yp2)
+            rows = slice(cut, None) if way else slice(0, cut)
+
+            def at(distance):
+                return (y + (NY - distance if way else distance)) % NY
+
+            def go(slot, src, dst, to):
+                copies[key, way, slot] = send(src, dst, send_sem(way, slot), recv_sem(way, slot), {"y": to})
+
+            if step == 0:
+                far = part(at(4), rows)
+                go(0, far, landing(way, 0, slice(0, far.shape[-2])), two)
+                go(1, part(at(3)), landing(way, 1), one)
+                go(2, part(at(1)), landing(way, 2), one)
+                continue
+            copies[key, way, 0].wait_recv()
+            copies[key, way, 1].wait_recv()
+            second = part(at(2))
+            second[...] += landing(way, 1)[...]
+            half_of = part(at(2), rows)
+            half_of[...] += landing(way, 0, slice(0, half_of.shape[-2]))[...]
+            go(3, second, landing(way, 3), two)
 
     yc = {}
 
-    def y_send_part(pair, way, step, src, dst):
-        to = ym if way else yp
-        yc[pair, way, step] = send(
-            src, dst, y_send.at[pair, way, step], y_recv.at[pair, way, step], {"y": to}
-        )
-
     def y_step(pair, step):
-        for way in range(2):
-            ahead = (mine + (4 + step if way else 4 - step)) % NY
-            rows = slice(CUT, ROWS) if way else slice(0, CUT)
-            size = ROWS - CUT if way else CUT
-            if step == 0:
-                y_send_part(pair, way, 0, total.at[pair, ahead, rows], yr.at[pair, way, 0, 0:size])
-                continue
-            yc[pair, way, step - 1].wait_recv()
-            if step == 1:
-                total[pair, ahead, rows] += yr[pair, way, 0, 0:size]
-            else:
-                total[pair, ahead] += yr[pair, way, step - 1]
-            y_send_part(pair, way, step, total.at[pair, ahead], yr.at[pair, way, step])
+        y_ways(
+            pair,
+            yc,
+            lambda place, rows=slice(0, ROWS): total.at[pair, place, slice(rows.start, rows.stop or ROWS)],
+            lambda way, slot, rows=slice(0, ROWS): yr.at[pair, way, slot, rows],
+            lambda way, slot: y_send.at[pair, way, slot],
+            lambda way, slot: y_recv.at[pair, way, slot],
+            CUT,
+            step,
+        )
 
     w, v = (w0, w1, w2), (v0, v1, v2)
     wc = {}
 
     def w_step(group, step):
-        for way in range(2):
-            ahead = (y + (4 + step if way else 4 - step)) % NY
-            rows = slice(REST_CUT, REST) if way else slice(0, REST_CUT)
-            size = REST - REST_CUT if way else REST_CUT
-            sems = (w_send.at[group, way, step], w_recv.at[group, way, step], {"y": ym if way else yp})
-            if step == 0:
-                wc[group, way, 0] = send(
-                    w[group].at[ahead, :, rows], v[group].at[way, 0, :, 0:size], *sems
-                )
-                continue
-            wc[group, way, step - 1].wait_recv()
-            if step == 1:
-                w[group][ahead, :, rows] += v[group][way, 0, :, 0:size]
-            else:
-                w[group][ahead] += v[group][way, step - 1]
-            wc[group, way, step] = send(w[group].at[ahead], v[group].at[way, step], *sems)
+        y_ways(
+            group,
+            wc,
+            lambda place, rows=slice(0, REST): w[group].at[place, :, slice(rows.start, rows.stop or REST)],
+            lambda way, slot, rows=slice(0, REST): v[group].at[way, slot, :, rows],
+            lambda way, slot: w_send.at[group, way, slot],
+            lambda way, slot: w_recv.at[group, way, slot],
+            REST_CUT,
+            step,
+        )
 
     def rest_copy(pair, jb, ih):
         k = block_of(pair, jb, ih)
@@ -290,10 +304,12 @@
 
     def w_deliver(group):
         for way in range(2):
+            wc[group, way, 2].wait_recv()
             wc[group, way, 3].wait_recv()
         for place, (pair, jb, ih) in enumerate(GROUPS[group]):
             k = block_of(pair, jb, ih)
-            rest[k] = w[group][y, place] + v[group][0, 3, place] + v[group][1, 3, place]
+            near = v[group][0, 2, place] + v[group][1, 2, place]
+            rest[k] = w[group][y, place] + near + (v[group][0, 3, place] + v[group][1, 3, place])
             if ih:
                 rest_copy(pair, jb, ih).start()
                 continue
@@ -332,8 +348,9 @@
 
     def deliver(pair):
         for way in range(2):
+            yc[pair, way, 2].wait_recv()
             yc[pair, way, 3].wait_recv()
-        done = total[pair, mine] + yr[pair, 0, 3] + yr[pair, 1, 3]
+        done = total[pair, y] + (yr[pair, 0, 2] + yr[pair, 1, 2]) + (yr[pair, 0, 3] + yr[pair, 1, 3])
         for part in range(2):
             if part:
                 fs[pair, 1, 0 : LEAD - OWN] = done[OWN:LEAD]
@@ -393,77 +410,70 @@
         spread_second = jnp.sqrt(square_second - mean_second * mean_second + EPS)
         out_ref[pair] = (both[0:OWN] / count - mean_second * mean_first) / (spread_second * spread_first)
 
+    def enter():
+        pl.semaphore_wait(barrier, 15 - at_home.astype(jnp.int32) - rest_home.astype(jnp.int32))
+
     for load in loads:
         load.wait()
     pick_first(0)
-    pl.semaphore_wait(barrier, 13 - at_home.astype(jnp.int32) - rest_home.astype(jnp.int32))
+    enter()
     offer(0, "a")
     offer(0, "p")
     pick_second(0)
     offer(0, "b")
     offer(0, "s")
-    arrive(0, "p")
-    multiply(0, 0, 0)
     pick_first(1)
     offer(1, "a")
     offer(1, "p")
-    pass_on(0, 0, 0)
     pick_second(1)
     offer(1, "b")
     offer(1, "s")
     arrive(1, "p")
     multiply(1, 0, 0)
+    arrive(0, "p")
+    multiply(0, 0, 0)
     w_step(0, 0)
+    pass_on(1, 0, 0)
     forward(0)
-    pass_on(1, 0, 0)
+    pass_on(0, 0, 0)
     w_step(0, 1)
+    arrive(0, "ap")
+    multiply(0, 0, 1)
     arrive(0, "b", "s")
     multiply(0, 1, 0)
-    w_step(0, 2)
-    arrive(0, "ap")
-    multiply(0, 0, 1)
     multiply(0, 1, 1)
+    collect(0, 0, 0)
+    collect(1, 0, 0)
     w_step(1, 0)
+    pass_on(0, 0, 1)
+    w_deliver(0)
     pass_on(0, 1, 0)
-    w_step(0, 3)
-    pass_on(0, 0, 1)
+    forward(1)
     pass_on(0, 1, 1)
     w_step(1, 1)
-    collect(0, 0, 0)
-    collect(1, 0, 0)
-    w_deliver(0)
-    forward(1)
-    collect(0, 1, 0)
-    w_step(1, 2)
+    arrive(1, "ap")
+    multiply(1, 0, 1)
     arrive(1, "b", "s")
     multiply(1, 1, 0)
-    collect(0, 0, 1)
-    arrive(1, "ap")
-    multiply(1, 0, 1)
     multiply(1, 1, 1)
     w_step(2, 0)
+    collect(0, 1, 0)
+    collect(0, 1, 1)
+    collect(0, 0, 1)
+    y_step(0, 0)
+    pass_on(1, 0, 1)
+    w_deliver(1)
     pass_on(1, 1, 0)
-    collect(0, 1, 1)
-    y_step(0, 0)
-    w_step(1, 3)
-    pass_on(1, 0, 1)
     pass_on(1, 1, 1)
     w_step(2, 1)
-    y_step(0, 1)
-    w_deliver(1)
+    collect(1, 0, 1)
     collect(1, 1, 0)
-    collect(1, 0, 1)
     collect(1, 1, 1)
     y_step(1, 0)
-    w_step(2, 2)
-    y_step(0, 2)
+    y_step(0, 1)
+    w_deliver(2)
     y_step(1, 1)
-    w_step(2, 3)
-    y_step(0, 3)
-    y_step(1, 2)
-    w_deliver(2)
     deliver(0)
-    y_step(1, 3)
     deliver(1)
     receive(0)
     receive(1)

time: 93.3 us -> 90.6 us (0.971)
  Pallas kernels: 91.5 us -> 88.8 us
    pallas_call x1, Pallas kernels: 91.5 us -> 88.8 us  [cross(): pl.pallas_call(cross_kernel, out_shape=jax.ShapeDtypeStruct((PAIRS, OWN,...]
where the time goes in v4:
time: 90.6 us; the launch traced here: 90.3 us
  Pallas kernels  88.8 us (98%)
  local copies, waits for them, and re-layouts  1.47 us (2%)
    pallas_call x1, Pallas kernels, cross(): pl.pallas_call(cross_kernel, out_shape=jax.ShapeDtypeStruct((PAIRS, OWN,...  88.8 us

profile of v4, /device:TPU:6, one launch (start us, length us, event | category | flops | bytes accessed | tf_op | source)
XLA Modules:
  0.0 90.3 jit_solution(2918072069411026454)
XLA Ops:
  0.0 88.8 %cross.1 = f32[2,32,256]{2,1,0:T(8,128)} custom-call(s32[2,2]{1,0:T(2,128)} %pair_ref.1, s32[40,128]{1,0:T(8,128)} %bitcast.4, s32[40,128]{1,0:T(8,128)} %bitcast.5, bf16[5120,256]{1,0:T(8,128)(2,1)} %emb_ref.1), custom_call_target="tpu_custom_call" | custom-call | tf_op jit(solution)/shard_map/cross/pallas_call | solution.py:501
  88.8 1.5 %copy.6 = f32[2,256,32]{1,2,0:T(8,128)} copy(f32[2,256,32]{1,2,0:T(8,128)} %bitcast.3) | data formatting | bytes 131072

commit v5 on v4

--- a/solution.py
+++ b/solution.py
@@ -47,8 +47,8 @@
     pair_ref, image_ref, view_ref, emb_ref, out_ref,
     emb, acc, found, counts, x1_ref, x2_ref, stat_ref,
     x1p, x1a, x1ap, x2b, statb, x1stat, cb, relay_p, relay_m, from_m, from_p, total, yr, fs, fr,
-    w0, w1, w2, v0, v1, v2, rest, rest_in,
-    emb_sem, z_send, z_recv, x_send, x_recv, y_send, y_recv, f_send, f_recv, w_send, w_recv, r_send, r_recv,
+    w0, w1, w2, v0, v1, v2, rest, rest_in, u0, u1, u2, g0, g1, g2,
+    emb_sem, z_send, z_recv, x_send, x_recv, y_send, y_recv, f_send, f_recv, w_send, w_recv, r_send, r_recv, g_send, g_recv,
 ):
     y, x, zl, h, core = [lax.axis_index(axis) for axis in AXES]
     plane_a = h + 1 - 2 * (h % 2)
@@ -72,6 +72,8 @@
     src_y = place_of(src_h, src_core, src_jb, src_ih, core)
     rest_y = 2 * x + core
     rest_home = (rest_y == y) & (src_h == h) & (zl == 1)
+    hub = y // 2
+    at_hub = x == hub
 
     loads = []
     for step in range(STEPS):
@@ -80,7 +82,7 @@
         loads[-1].start()
 
     barrier = pltpu.get_barrier_semaphore()
-    for peer in ({"x": xp}, {"x": xm}, {"y": yp}, {"y": ym}, {"y": yp2}, {"y": ym2}, {"zh": plane_a}, {"zh": plane_b}, {"core": other}):
+    for peer in ({"x": xp}, {"x": xm}, {"x": xa}, {"y": yp}, {"y": ym}, {"y": yp2}, {"y": ym2}, {"zh": plane_a}, {"zh": plane_b}, {"core": other}):
         pl.semaphore_signal(barrier, inc=1, device_id=peer, device_id_type=MESH)
     for part in range(2):
 
@@ -93,17 +95,16 @@
                 device_id_type=MESH,
             )
 
-    for from_x in range(NX):
-        for part in range(2):
-
-            @pl.when((zl == 1) & jnp.logical_not(rest_home & (x == from_x) & (zl == part)))
-            def _():
-                pl.semaphore_signal(
-                    barrier,
-                    inc=1,
-                    device_id={"y": rest_y, "x": from_x, "zl": part, "zh": src_h, "core": src_core},
-                    device_id_type=MESH,
-                )
+    for part in range(2):
+
+        @pl.when((zl == 1) & jnp.logical_not(rest_home & (zl == part)))
+        def _():
+            pl.semaphore_signal(
+                barrier,
+                inc=1,
+                device_id={"y": rest_y, "zl": part, "zh": src_h, "core": src_core},
+                device_id_type=MESH,
+            )
 
     sent = []
 
@@ -289,12 +290,12 @@
         k = block_of(pair, jb, ih)
         return pltpu.make_async_remote_copy(
             src_ref=rest.at[k],
-            dst_ref=rest_in.at[pair, x, zl],
+            dst_ref=rest_in.at[pair, zl],
             send_sem=r_send.at[k],
-            recv_sem=r_recv.at[pair, x, zl],
+            recv_sem=r_recv.at[pair, zl],
             device_id={
                 "y": 2 * (plane_b if jb else h) + core,
-                "x": y // 2,
+                "x": hub,
                 "zl": 1,
                 "zh": plane_a if ih else h,
                 "core": y % 2,
@@ -302,49 +303,72 @@
             device_id_type=MESH,
         )
 
-    def w_deliver(group):
+    u, gx = (u0, u1, u2), (g0, g1, g2)
+
+    def gather_copy(group, from_x, to=hub):
+        return pltpu.make_async_remote_copy(
+            src_ref=u[group],
+            dst_ref=gx[group].at[from_x],
+            send_sem=g_send.at[group],
+            recv_sem=g_recv.at[group, from_x],
+            device_id={"x": to},
+            device_id_type=MESH,
+        )
+
+    def w_gather(group):
         for way in range(2):
             wc[group, way, 2].wait_recv()
             wc[group, way, 3].wait_recv()
-        for place, (pair, jb, ih) in enumerate(GROUPS[group]):
-            k = block_of(pair, jb, ih)
-            near = v[group][0, 2, place] + v[group][1, 2, place]
-            rest[k] = w[group][y, place] + near + (v[group][0, 3, place] + v[group][1, 3, place])
-            if ih:
-                rest_copy(pair, jb, ih).start()
-                continue
-            same = rest_home & (src_jb == jb)
-
-            @pl.when(same)
-            def _():
-                rest_in[pair, x, zl] = rest[k]
-
-            @pl.when(jnp.logical_not(same))
-            def _():
-                rest_copy(pair, jb, ih).start()
+        near = v[group][0, 2] + v[group][1, 2]
+        u[group][...] = w[group][y] + near + (v[group][0, 3] + v[group][1, 3])
+
+        @pl.when(jnp.logical_not(at_hub))
+        def _():
+            gather_copy(group, x).start()
+
+    def w_deliver(group):
+        @pl.when(at_hub)
+        def _():
+            for from_x in range(NX):
+
+                @pl.when(x != from_x)
+                def _():
+                    gather_copy(group, from_x, xp).wait_recv()
+
+            summed = u[group][...] + gx[group][xa] + (gx[group][xp] + gx[group][xm])
+            for place, (pair, jb, ih) in enumerate(GROUPS[group]):
+                rest[block_of(pair, jb, ih)] = summed[place]
+            for pair, jb, ih in GROUPS[group]:
+                if ih:
+                    rest_copy(pair, jb, ih).start()
+                    continue
+                same = rest_home & (src_jb == jb)
+
+                @pl.when(same)
+                def _():
+                    rest_in[pair, zl] = rest[block_of(pair, jb, ih)]
+
+                @pl.when(jnp.logical_not(same))
+                def _():
+                    rest_copy(pair, jb, ih).start()
 
     def rest_receive(pair):
         @pl.when(zl == 1)
         def _():
-            for from_x in range(NX):
-                for part in range(2):
-
-                    @pl.when(jnp.logical_not(rest_home & (x == from_x) & (zl == part)))
-                    def _():
-                        pltpu.make_async_remote_copy(
-                            src_ref=rest.at[0],
-                            dst_ref=rest_in.at[pair, from_x, part],
-                            send_sem=r_send.at[0],
-                            recv_sem=r_recv.at[pair, from_x, part],
-                            device_id={"x": xp},
-                            device_id_type=MESH,
-                        ).wait_recv()
-
-            lead = OWN - REST
-            summed = rest_in[pair, 0, 0]
-            for slot in range(1, 2 * NX):
-                summed += rest_in[pair, slot // 2, slot % 2]
-            fr[pair, 0, lead:OWN] += summed
+            for part in range(2):
+
+                @pl.when(jnp.logical_not(rest_home & (zl == part)))
+                def _():
+                    pltpu.make_async_remote_copy(
+                        src_ref=rest.at[0],
+                        dst_ref=rest_in.at[pair, part],
+                        send_sem=r_send.at[0],
+                        recv_sem=r_recv.at[pair, part],
+                        device_id={"x": xp},
+                        device_id_type=MESH,
+                    ).wait_recv()
+
+            fr[pair, 0, OWN - REST : OWN] += rest_in[pair, 0] + rest_in[pair, 1]
 
     def deliver(pair):
         for way in range(2):
@@ -411,7 +435,8 @@
         out_ref[pair] = (both[0:OWN] / count - mean_second * mean_first) / (spread_second * spread_first)
 
     def enter():
-        pl.semaphore_wait(barrier, 15 - at_home.astype(jnp.int32) - rest_home.astype(jnp.int32))
+        owners = 4 * at_hub.astype(jnp.int32) - rest_home.astype(jnp.int32)
+        pl.semaphore_wait(barrier, 12 - at_home.astype(jnp.int32) + owners)
 
     for load in loads:
         load.wait()
@@ -422,60 +447,63 @@
     pick_second(0)
     offer(0, "b")
     offer(0, "s")
+    arrive(0, "p")
+    multiply(0, 0, 0)
     pick_first(1)
     offer(1, "a")
     offer(1, "p")
     pick_second(1)
     offer(1, "b")
     offer(1, "s")
+    pass_on(0, 0, 0)
     arrive(1, "p")
     multiply(1, 0, 0)
-    arrive(0, "p")
-    multiply(0, 0, 0)
     w_step(0, 0)
+    collect(0, 0, 0)
     pass_on(1, 0, 0)
     forward(0)
-    pass_on(0, 0, 0)
     w_step(0, 1)
     arrive(0, "ap")
     multiply(0, 0, 1)
     arrive(0, "b", "s")
+    multiply(0, 1, 1)
+    collect(1, 0, 0)
     multiply(0, 1, 0)
-    multiply(0, 1, 1)
-    collect(0, 0, 0)
-    collect(1, 0, 0)
     w_step(1, 0)
     pass_on(0, 0, 1)
-    w_deliver(0)
+    w_gather(0)
+    pass_on(0, 1, 1)
+    forward(1)
     pass_on(0, 1, 0)
-    forward(1)
-    pass_on(0, 1, 1)
     w_step(1, 1)
     arrive(1, "ap")
     multiply(1, 0, 1)
     arrive(1, "b", "s")
     multiply(1, 1, 0)
     multiply(1, 1, 1)
+    w_deliver(0)
+    collect(0, 0, 1)
     w_step(2, 0)
+    collect(0, 1, 1)
     collect(0, 1, 0)
-    collect(0, 1, 1)
-    collect(0, 0, 1)
     y_step(0, 0)
     pass_on(1, 0, 1)
-    w_deliver(1)
+    w_gather(1)
     pass_on(1, 1, 0)
     pass_on(1, 1, 1)
     w_step(2, 1)
     collect(1, 0, 1)
+    y_step(0, 1)
+    w_deliver(1)
     collect(1, 1, 0)
     collect(1, 1, 1)
     y_step(1, 0)
-    y_step(0, 1)
+    w_gather(2)
+    deliver(0)
+    y_step(1, 1)
     w_deliver(2)
-    y_step(1, 1)
-    deliver(0)
+    receive(0)
     deliver(1)
-    receive(0)
     receive(1)
 
     for copy in sent:
@@ -486,10 +514,15 @@
             @pl.when(jnp.logical_not(at_home & (zl == part)))
             def _():
                 final_copy(pair, part).wait_send()
-    for group in GROUPS:
-        for pair, jb, ih in group:
-
-            @pl.when(jnp.logical_not(rest_home & (src_jb == jb) & (ih == 0)))
+    for group, blocks in enumerate(GROUPS):
+
+        @pl.when(jnp.logical_not(at_hub))
+        def _():
+            gather_copy(group, x).wait_send()
+
+        for pair, jb, ih in blocks:
+
+            @pl.when(at_hub & jnp.logical_not(rest_home & (src_jb == jb) & (ih == 0)))
             def _():
                 rest_copy(pair, jb, ih).wait_send()
 
@@ -529,7 +562,9 @@
             *(pltpu.VMEM((NY, len(blocks_of), REST, WIDTH), F32) for blocks_of in GROUPS),
             *(pltpu.VMEM((2, 4, len(blocks_of), REST, WIDTH), F32) for blocks_of in GROUPS),
             pltpu.VMEM((blocks, REST, WIDTH), F32),
-            pltpu.VMEM((PAIRS, NX, 2, REST, WIDTH), F32),
+            pltpu.VMEM((PAIRS, 2, REST, WIDTH), F32),
+            *(pltpu.VMEM((len(blocks_of), REST, WIDTH), F32) for blocks_of in GROUPS),
+            *(pltpu.VMEM((NX, len(blocks_of), REST, WIDTH), F32) for blocks_of in GROUPS),
             dma((STEPS,)),
             dma((PAIRS, 5)),
             dma((PAIRS, 5)),
@@ -542,7 +577,9 @@
             dma((len(GROUPS), 2, 4)),
             dma((len(GROUPS), 2, 4)),
             dma((blocks,)),
-            dma((PAIRS, NX, 2)),
+            dma((PAIRS, 2)),
+            dma((len(GROUPS),)),
+            dma((len(GROUPS), NX)),
         ],
         compiler_params=pltpu.CompilerParams(collective_id=0, has_side_effects=True),
         name="cross",

time: 90.6 us -> 88.9 us (0.981)
  the two profiles are of different devices: /device:TPU:6 before, /device:TPU:4 now
where the time goes in v5:
time: 88.9 us; the launch traced here: 88.7 us
  Pallas kernels  87.2 us (98%)
  local copies, waits for them, and re-layouts  1.47 us (2%)
    pallas_call x1, Pallas kernels, cross(): pl.pallas_call(cross_kernel, out_shape=jax.ShapeDtypeStruct((PAIRS, OWN,...  87.2 us

profile of v5, /device:TPU:4, one launch (start us, length us, event | category | flops | bytes accessed | tf_op | source)
XLA Modules:
  0.0 88.7 jit_solution(574206192420899727)
XLA Ops:
  0.0 87.2 %cross.1 = f32[2,32,256]{2,1,0:T(8,128)} custom-call(s32[2,2]{1,0:T(2,128)} %pair_ref.1, s32[40,128]{1,0:T(8,128)} %bitcast.4, s32[40,128]{1,0:T(8,128)} %bitcast.5, bf16[5120,256]{1,0:T(8,128)(2,1)} %emb_ref.1), custom_call_target="tpu_custom_call" | custom-call | tf_op jit(solution)/shard_map/cross/pallas_call | solution.py:534
  87.2 1.5 %copy.6 = f32[2,256,32]{1,2,0:T(8,128)} copy(f32[2,256,32]{1,2,0:T(8,128)} %bitcast.3) | data formatting | bytes 131072

commit v6 on v5

--- a/solution.py
+++ b/solution.py
@@ -14,12 +14,13 @@
 NX, NY = 4, 8
 BLOCK = 64
 STAT = 8
-LEAD = 40
+LEAD = 48
 REST = BLOCK - LEAD
 ROWS = LEAD + STAT
 PART = OWN + STAT
-CUT = 24
-REST_CUT = 16
+SENT = (PART, STAT + LEAD - OWN)
+CUT = 32
+REST_CUT = 8
 GROUPS = (
     ((0, 0, 0), (1, 0, 0)),
     ((0, 1, 0), (0, 0, 1), (0, 1, 1)),
@@ -368,7 +369,8 @@
                         device_id_type=MESH,
                     ).wait_recv()
 
-            fr[pair, 0, OWN - REST : OWN] += rest_in[pair, 0] + rest_in[pair, 1]
+            fr[pair, 0, SENT[1] : PART] = rest_in[pair, 0] + rest_in[pair, 1]
+            fr[pair, 1, SENT[1] : PART] = jnp.zeros((REST, WIDTH), F32)
 
     def deliver(pair):
         for way in range(2):
@@ -376,17 +378,13 @@
             yc[pair, way, 3].wait_recv()
         done = total[pair, y] + (yr[pair, 0, 2] + yr[pair, 1, 2]) + (yr[pair, 0, 3] + yr[pair, 1, 3])
         for part in range(2):
-            if part:
-                fs[pair, 1, 0 : LEAD - OWN] = done[OWN:LEAD]
-                fs[pair, 1, LEAD - OWN : OWN] = jnp.zeros((REST, WIDTH), F32)
-            else:
-                fs[pair, 0, 0:OWN] = done[0:OWN]
-            fs[pair, part, OWN:PART] = done[LEAD:ROWS]
+            fs[pair, part, 0:STAT] = done[LEAD:ROWS]
+            fs[pair, part, STAT : SENT[part]] = done[OWN:LEAD] if part else done[0:OWN]
             same = at_home & (zl == part)
 
             @pl.when(same)
             def _():
-                fr[pair, zl] = fs[pair, part]
+                fr[pair, zl, 0 : SENT[part]] = fs[pair, part, 0 : SENT[part]]
 
             @pl.when(jnp.logical_not(same))
             def _():
@@ -394,8 +392,8 @@
 
     def final_copy(pair, part):
         return pltpu.make_async_remote_copy(
-            src_ref=fs.at[pair, part],
-            dst_ref=fr.at[pair, zl],
+            src_ref=fs.at[pair, part, 0 : SENT[part]],
+            dst_ref=fr.at[pair, zl, 0 : SENT[part]],
             send_sem=f_send.at[pair, part],
             recv_sem=f_recv.at[pair, zl],
             device_id={"y": owner_y, "zl": part, "zh": owner_h, "core": half},
@@ -405,20 +403,22 @@
     def receive(pair):
         for part in range(2):
 
-            @pl.when(jnp.logical_not(at_home & (zl == part)))
-            def _():
-                pltpu.make_async_remote_copy(
-                    src_ref=fs.at[pair, part],
-                    dst_ref=fr.at[pair, part],
-                    send_sem=f_send.at[pair, part],
-                    recv_sem=f_recv.at[pair, part],
-                    device_id={"y": owner_y, "zl": part, "zh": owner_h, "core": half},
-                    device_id_type=MESH,
-                ).wait_recv()
+            for own in range(2):
+
+                @pl.when((zl == own) & jnp.logical_not(at_home & (zl == part)))
+                def _():
+                    pltpu.make_async_remote_copy(
+                        src_ref=fs.at[pair, part, 0 : SENT[own]],
+                        dst_ref=fr.at[pair, part, 0 : SENT[own]],
+                        send_sem=f_send.at[pair, part],
+                        recv_sem=f_recv.at[pair, part],
+                        device_id={"x": xp},
+                        device_id_type=MESH,
+                    ).wait_recv()
 
         rest_receive(pair)
         both = fr[pair, 0] + fr[pair, 1]
-        count = both[OWN + 4 : OWN + 5, 0:1]
+        count = both[4 : 5, 0:1]
         lane = lax.broadcasted_iota(jnp.int32, (OWN, WIDTH), 1)
         row = lax.broadcasted_iota(jnp.int32, (OWN, WIDTH), 0)
         own = lane == row + (x * BLOCK + zl * OWN)
@@ -426,13 +426,13 @@
         def column(line):
             return jnp.sum(jnp.where(own, line, 0.0), axis=1, keepdims=True)
 
-        mean_first = both[OWN : OWN + 1] / count
-        square_first = both[OWN + 1 : OWN + 2] / count
-        mean_second = column(both[OWN + 2 : OWN + 3]) / count
-        square_second = column(both[OWN + 3 : OWN + 4]) / count
+        mean_first = both[0:1] / count
+        square_first = both[1 : 2] / count
+        mean_second = column(both[2 : 3]) / count
+        square_second = column(both[3 : 4]) / count
         spread_first = jnp.sqrt(square_first - mean_first * mean_first + EPS)
         spread_second = jnp.sqrt(square_second - mean_second * mean_second + EPS)
-        out_ref[pair] = (both[0:OWN] / count - mean_second * mean_first) / (spread_second * spread_first)
+        out_ref[pair] = (both[STAT:PART] / count - mean_second * mean_first) / (spread_second * spread_first)
 
     def enter():
         owners = 4 * at_hub.astype(jnp.int32) - rest_home.astype(jnp.int32)

time: 88.9 us -> 86.2 us (0.970)
  Pallas kernels: 87.2 us -> 84.5 us
    pallas_call x1, Pallas kernels: 87.2 us -> 84.5 us  [cross(): pl.pallas_call(cross_kernel, out_shape=jax.ShapeDtypeStruct((PAIRS, OWN,...]
where the time goes in v6:
time: 86.2 us; the launch traced here: 86 us
  Pallas kernels  84.5 us (98%)
  local copies, waits for them, and re-layouts  1.47 us (2%)
    pallas_call x1, Pallas kernels, cross(): pl.pallas_call(cross_kernel, out_shape=jax.ShapeDtypeStruct((PAIRS, OWN,...  84.5 us

profile of v6, /device:TPU:4, one launch (start us, length us, event | category | flops | bytes accessed | tf_op | source)
XLA Modules:
  0.0 86.0 jit_solution(3349514768011403055)
XLA Ops:
  0.0 84.5 %cross.1 = f32[2,32,256]{2,1,0:T(8,128)} custom-call(s32[2,2]{1,0:T(2,128)} %pair_ref.1, s32[40,128]{1,0:T(8,128)} %bitcast.4, s32[40,128]{1,0:T(8,128)} %bitcast.5, bf16[5120,256]{1,0:T(8,128)(2,1)} %emb_ref.1), custom_call_target="tpu_custom_call" | custom-call | tf_op jit(solution)/shard_map/cross/pallas_call | solution.py:534
  84.5 1.5 %copy.6 = f32[2,256,32]{1,2,0:T(8,128)} copy(f32[2,256,32]{1,2,0:T(8,128)} %bitcast.3) | data formatting | bytes 131072

commit v7 on v6

--- a/solution.py
+++ b/solution.py
@@ -76,11 +76,12 @@
     hub = y // 2
     at_hub = x == hub
 
-    loads = []
+    def load(step):
+        rows = pl.ds(pl.multiple_of(step * SLOTS, SLOTS), SLOTS)
+        return pltpu.make_async_copy(emb_ref.at[rows], emb.at[rows], emb_sem.at[step])
+
     for step in range(STEPS):
-        rows = slice(step * SLOTS, (step + 1) * SLOTS)
-        loads.append(pltpu.make_async_copy(emb_ref.at[rows], emb.at[rows], emb_sem.at[step]))
-        loads[-1].start()
+        load(step).start()
 
     barrier = pltpu.get_barrier_semaphore()
     for peer in ({"x": xp}, {"x": xm}, {"x": xa}, {"y": yp}, {"y": ym}, {"y": yp2}, {"y": ym2}, {"zh": plane_a}, {"zh": plane_b}, {"core": other}):
@@ -143,6 +144,8 @@
             found[...] = jnp.zeros_like(found)
 
         def step(index, carry):
+            if (pair, side) == (0, 0):
+                load(index).wait()
             key = image_ref[pl.ds(pl.multiple_of(index * TILE, TILE), TILE), :] * VIEW_STRIDE
             key += view_ref[pl.ds(pl.multiple_of(index * TILE, TILE), TILE), :]
             keys = [key[row : row + 1, :] for row in range(TILE)]
@@ -438,8 +441,6 @@
         owners = 4 * at_hub.astype(jnp.int32) - rest_home.astype(jnp.int32)
         pl.semaphore_wait(barrier, 12 - at_home.astype(jnp.int32) + owners)
 
-    for load in loads:
-        load.wait()
     pick_first(0)
     enter()
     offer(0, "a")

time: 86.2 us -> 86.3 us (level)
  no operation moved by 1% of the time
where the time goes in v7:
time: 86.3 us; the launch traced here: 86.1 us
  Pallas kernels  84.6 us (98%)
  local copies, waits for them, and re-layouts  1.47 us (2%)
    pallas_call x1, Pallas kernels, cross(): pl.pallas_call(cross_kernel, out_shape=jax.ShapeDtypeStruct((PAIRS, OWN,...  84.6 us

profile of v7, /device:TPU:4, one launch (start us, length us, event | category | flops | bytes accessed | tf_op | source)
XLA Modules:
  0.0 86.1 jit_solution(2592307659083195443)
XLA Ops:
  0.0 84.6 %cross.1 = f32[2,32,256]{2,1,0:T(8,128)} custom-call(s32[2,2]{1,0:T(2,128)} %pair_ref.1, s32[40,128]{1,0:T(8,128)} %bitcast.4, s32[40,128]{1,0:T(8,128)} %bitcast.5, bf16[5120,256]{1,0:T(8,128)(2,1)} %emb_ref.1), custom_call_target="tpu_custom_call" | custom-call | tf_op jit(solution)/shard_map/cross/pallas_call | solution.py:535
  84.6 1.5 %copy.6 = f32[2,256,32]{1,2,0:T(8,128)} copy(f32[2,256,32]{1,2,0:T(8,128)} %bitcast.3) | data formatting | bytes 131072
